TPU v7x, 128 devices: a whole 4x4x4 slice. The times are simulated.
128 devices in a mesh: dp: 32 (over y_hi, x, z), head: 4 (over y_lo, core).
Axes of the slice: x: 4, y: 4 (y_hi: 2, y_lo: 2; y = y_hi * 2 + y_lo), z: 4, core: 2. Of those that a mesh axis runs over, the one named last changes fastest.
Arguments:
- residual: bfloat16 [128, 4096], P('dp', 'head'), may hold values from -6 to 6
- query: bfloat16 [128, 32, 128], P('dp', 'head'), may hold values from -4.5 to 4.5
- fresh_token_keys: bfloat16 [128, 8, 128], P('dp', 'head'), may hold values from -4.5 to 4.5
- value_new: bfloat16 [128, 8, 128], P('dp', 'head'), may hold values from -24 to 24
- key_cache: bfloat16 [128, 8, 2048, 128], P('dp', 'head'), may hold values from -6 to 6
- value_cache: bfloat16 [128, 8, 2048, 128], P('dp', 'head'), may hold values from -6 to 6
- lengths: int32 [128], P('dp'), may hold values from 1024 to 2048, as said below
- pages: int32 [128, 8, 64], P('dp', 'head'), may hold values from 0 to 127, as said below
- w_out: bfloat16 [4096, 4096], P('head', 'dp'), may hold values from -0.75 to 0.75
- norm_gain: float32 [4096], P('head'), may hold values from 0.5 to 1.5
- expert_ids: int32 [128, 2], P('dp'), may hold values from 0 to 7, all different within a row; in each aligned block of 4 rows (0 to 3, 4 to 7, ...) at most 2 rows name the same one
- gate_weights: float32 [128, 2], P('dp'), may hold values from 0.1 to 1
- w_in: bfloat16 [32, 2, 4096, 1792], P('dp', None, None, 'head'), may hold values from -0.09375 to 0.09375
- w_down: bfloat16 [32, 1792, 4096], P('dp', 'head'), may hold values from -0.0625 to 0.0625
Outputs:
- layer_out: bfloat16 [128, 4096], P('dp', 'head')
Inputs may be any that keep to these rules, and one draw needn't show every extreme that they name: `lengths`: each request's length; some request has exactly 2048 and some exactly 1024. `pages`: for each request and key head, 64 distinct page numbers, all below ceil(length / 16), always including the page that holds the request's last cached token; in no fixed order. `expert_ids`: per token 2 distinct experts; among the 4 tokens of one dp index no expert is named more than 2 times.
All inputs are finite; a program needn't handle non-finite values.
Results may differ from a plain program's by a relative error of at most 0.012.
Values may be sent and summed in bfloat16 or wider, within the bound.
A program may use at most 64 MiB of HBM per device.

v0:
```python
import jax
import jax.numpy as jnp
from jax import lax
from jax.sharding import PartitionSpec as P

EXPERTS = 8
TOP = 2
PAGE = 16
MOST = 2


EPSILON = 1e-05


def laid_out(parts, dim):
    dims = list(parts.shape[1:])
    dims[dim] *= parts.shape[0]
    return jnp.moveaxis(parts, 0, dim).reshape(dims)


def copy_for_each(value, axis):
    copies = jnp.broadcast_to(value, (lax.axis_size(axis), *value.shape))
    return lax.all_to_all(copies, axis, split_axis=0, concat_axis=0, tiled=True)


def collect(value, axis, dim):
    return laid_out(copy_for_each(value, axis), dim)


def in_blocks(value, dim, peers):
    before, after = (value.shape[:dim], value.shape[dim + 1 :])
    return jnp.moveaxis(value.reshape(*before, peers, -1, *after), dim, 0)


def sent_and_summed(value, axis, dim):
    parts = in_blocks(value, dim, lax.axis_size(axis))
    arrived = lax.all_to_all(parts, axis, split_axis=0, concat_axis=0, tiled=True)
    return arrived.astype(jnp.float32).sum(axis=0)


def rows_first(arrays, axis, dims):
    turned = [jnp.moveaxis(a, dim, 0) for a, dim in zip(arrays, dims)]
    widths = [t[0].size for t in turned]
    both = jnp.concatenate([t.reshape(-1, w) for t, w in zip(turned, widths)], axis=1)
    whole = lax.all_gather(both, axis, axis=0, tiled=True)
    parts = jnp.split(whole, [sum(widths[:k]) for k in range(1, len(widths))], axis=1)
    return tuple(
        (
            jnp.moveaxis(b.reshape(-1, *t.shape[1:]), 0, dim)
            for b, t, dim in zip(parts, turned, dims)
        )
    )


def shards(
    residual,
    query,
    fresh_token_keys,
    value_new,
    key_cache,
    value_cache,
    lengths,
    pages,
    w_out,
    norm_gain,
    expert_ids,
    gate_weights,
    w_in,
    w_down,
):
    tok_rows = query.shape[0]
    head_local = query.shape[1]
    head_dim = query.shape[2]
    kv_local = key_cache.shape[1]
    cache_len = key_cache.shape[2]
    page_total = cache_len // PAGE
    group_member_count = head_local // kv_local
    page_numbers = jnp.arange(page_total, dtype=jnp.int32)
    page_chosen = jnp.any(pages[:, :, :, None] == page_numbers[None, None, None, :], axis=2)
    position_chosen = jnp.broadcast_to(
        page_chosen[:, :, :, None], (tok_rows, kv_local, page_total, PAGE)
    ).reshape(tok_rows, kv_local, cache_len)
    position_ids = jnp.arange(cache_len, dtype=jnp.int32)
    in_range = (position_chosen & (position_ids[None, None, :] < lengths[:, None, None]))[
        :, :, None, :
    ]
    grouped_rows = query.reshape(tok_rows, kv_local, group_member_count, head_dim)
    score_scale = head_dim ** (-0.5)
    scores = (
        jnp.einsum("bkgd,bksd->bkgs", grouped_rows, key_cache, preferred_element_type=jnp.float32)
        * score_scale
    )
    own_score = (
        jnp.einsum(
            "luxe,lue->lux", grouped_rows, fresh_token_keys, preferred_element_type=jnp.float32
        )
        * score_scale
    )
    masked = jnp.where(in_range, scores, -1e30)
    row_top = jnp.maximum(jnp.max(masked, axis=-1), own_score)
    expo = jnp.where(in_range, jnp.exp(scores - row_top[..., None]), 0.0)
    own_expo = jnp.exp(own_score - row_top)
    denominator = jnp.sum(expo, axis=-1) + own_expo
    weights = (expo / denominator[..., None]).astype(jnp.bfloat16)
    own_weight = (own_expo / denominator).astype(jnp.bfloat16)
    attended = jnp.einsum(
        "bkgs,bksd->bkgd", weights, value_cache, preferred_element_type=jnp.float32
    )
    attended = (
        attended
        + own_weight.astype(jnp.float32)[..., None] * value_new.astype(jnp.float32)[:, :, None, :]
    )
    attn_rows = attended.reshape(tok_rows, head_local * head_dim).astype(jnp.bfloat16)
    every_row = collect(attn_rows, "dp", 0)
    column_part = jnp.dot(every_row, w_out, preferred_element_type=jnp.float32)
    head_partial = lax.all_to_all(
        column_part.astype(jnp.bfloat16), "dp", split_axis=0, concat_axis=1, tiled=True
    ).astype(column_part.dtype)
    stream = residual.astype(jnp.float32) + sent_and_summed(
        head_partial.astype(jnp.bfloat16), "head", 1
    )
    whole_stream, whole_gain = rows_first((stream, norm_gain), "head", (1, 0))
    square_mean_value = jnp.mean(whole_stream * whole_stream, axis=-1)
    normed = (
        whole_stream * lax.rsqrt(square_mean_value + EPSILON)[:, None] * whole_gain[None, :]
    ).astype(jnp.bfloat16)
    group_count = lax.axis_size("dp") // EXPERTS
    assignments = tok_rows * TOP
    flat_ids = expert_ids.reshape(assignments)
    expert_range = jnp.arange(EXPERTS, dtype=jnp.int32)
    onehot = (flat_ids[:, None] == expert_range[None, :]).astype(jnp.int32)
    earlier = jnp.cumsum(onehot, axis=0) - onehot
    slot_index = jnp.sum(earlier * onehot, axis=1)
    target = flat_ids * MOST + slot_index
    placement_map = jnp.arange(EXPERTS * MOST, dtype=jnp.int32)[:, None] == target[None, :]
    token_map = jnp.any(placement_map.reshape(EXPERTS * MOST, tok_rows, TOP), axis=2)
    outgoing = jnp.dot(
        token_map.astype(jnp.bfloat16), normed, preferred_element_type=jnp.float32
    ).astype(jnp.bfloat16)
    width_of_row = outgoing.shape[1]
    outgoing = jnp.broadcast_to(
        outgoing.reshape(EXPERTS, 1, MOST, width_of_row), (EXPERTS, group_count, MOST, width_of_row)
    )
    outgoing = outgoing.reshape(EXPERTS * group_count, MOST, width_of_row)
    arrived = lax.all_to_all(outgoing, "dp", split_axis=0, concat_axis=0, tiled=True)
    senders, slot_count, feature_count = arrived.shape
    flat_rows = arrived.reshape(senders * slot_count, feature_count)
    gate_act = jnp.dot(flat_rows, w_in[0, 0], preferred_element_type=jnp.float32)
    up_act = jnp.dot(flat_rows, w_in[0, 1], preferred_element_type=jnp.float32)
    hidden = (jax.nn.silu(gate_act) * up_act).astype(jnp.bfloat16)
    slab_out = jnp.dot(hidden, w_down[0], preferred_element_type=jnp.float32).reshape(
        senders, slot_count, w_down.shape[2]
    )
    summed_total = sent_and_summed(slab_out.astype(jnp.bfloat16), "head", 2)
    returned = lax.all_to_all(
        summed_total.astype(jnp.bfloat16), "dp", split_axis=0, concat_axis=0, tiled=True
    ).astype(summed_total.dtype)
    local_width = returned.shape[2]
    per_expert = jnp.sum(returned.reshape(EXPERTS, group_count, MOST, local_width), axis=1).reshape(
        EXPERTS * MOST, local_width
    )
    weighted = jnp.where(placement_map, gate_weights.reshape(assignments)[None, :], 0.0)
    combine_map = jnp.sum(weighted.reshape(EXPERTS * MOST, tok_rows, TOP), axis=2)
    mixture = jnp.dot(
        combine_map.T,
        per_expert,
        precision=lax.Precision.HIGHEST,
        preferred_element_type=jnp.float32,
    )
    return (stream + mixture).astype(jnp.bfloat16)


def solution(mesh):
    in_specs = (
        P("dp", "head"),
        P("dp", "head", None),
        P("dp", "head", None),
        P("dp", "head", None),
        P("dp", "head", None, None),
        P("dp", "head", None, None),
        P("dp"),
        P("dp", "head", None),
        P("head", "dp"),
        P("head"),
        P("dp", None),
        P("dp", None),
        P("dp", None, None, "head"),
        P("dp", "head", None),
    )
    out_specs = P("dp", "head")
    return jax.shard_map(shards, mesh=mesh, in_specs=in_specs, out_specs=out_specs, check_vma=False)
```

profile of v0, /device:TPU:1, one launch (start us, length us, event | category | flops | bytes accessed | tf_op | source)
XLA Modules:
  0.0 112.0 jit_solution(9773123583154658244)
XLA Ops:
  0.0 0.0 copy-start
  0.0 0.0 copy-start.3
  0.0 0.9 fusion.15
  0.9 0.2 broadcast_in_dim.59
  1.1 0.3 reshape.115
  1.4 0.0 copy-start.6
  1.4 0.9 iota_compare_fusion.1
  2.4 1.1 fusion.27
  3.5 0.0 copy-start.4
  3.5 3.5 %select_reduce_fusion = (f32[4,2,4]{2,1,0:T(2,128)S(1)}, f32[4,2,4,2048]{3,2,1,0:T(4,128)S(1)}) fusion(pred[4,2,2048]{2,1,0:T(4,128)(4,1)S(1)} %copy.58, bf16[4,2,4,128]{3,2,1,0:T(4,128)(2,1)} %bitcast.66, bf16[4,2,2048,128]{3,2,1,0:T(8,128)(2,1)} %param.18), kind=kOutput, calls=%fused_computation.20 | convolution fusion | flops 16973792 | bytes 4481152 | tf_op jit(solution)/shard_map/bkgd,bksd->bkgs/dot_general | solution.py:90
  7.0 0.0 copy-start.1
  7.0 0.0 copy-start.2
  7.0 0.3 fusion.16
  7.3 0.0 copy-done.3
  7.3 0.0 copy-done.6
  7.4 0.7 fusion.14
  8.1 0.8 broadcast_in_dim.63
  8.9 11.3 %all-to-all-start = ((bf16[32,4,1024]{2,1,0:T(4,128)(2,1)}), bf16[32,4,1024]{2,1,0:T(4,128)(2,1)S(1)}, u32[]{:S(2)}, u32[]{:S(2)}) async-start(bf16[32,4,1024]{2,1,0:T(4,128)(2,1)} %broadcast_in_dim.63), calls=%async_computation | async-start | bytes 524288 | tf_op jit(solution)/shard_map/all_to_all | solution.py:23
  20.2 0.0 copy-done.4
  20.2 0.1 copy.61
  20.3 0.1 eq.47
  20.4 0.1 fusion.25
  20.5 0.2 select_reduce_fusion.2
  20.7 0.1 reduce_sum.71
  20.8 8.8 %all-to-all-done = bf16[32,4,1024]{2,1,0:T(4,128)(2,1)S(1)} async-done(((bf16[32,4,1024]{2,1,0:T(4,128)(2,1)}), bf16[32,4,1024]{2,1,0:T(4,128)(2,1)S(1)}, u32[]{:S(2)}, u32[]{:S(2)}) %all-to-all-start) | async-done | bytes 262176 | tf_op jit(solution)/shard_map/all_to_all | solution.py:23
  29.7 0.1 reshape.117
  29.7 0.0 copy-done
  29.7 0.8 convolution_convert_fusion.2
  30.6 4.2 %all-to-all-start.1 = ((bf16[32,4,128]{2,1,0:T(4,128)(2,1)}), bf16[32,4,128]{2,1,0:T(4,128)(2,1)S(1)}, u32[]{:S(2)}, u32[]{:S(2)}) async-start(bf16[32,4,128]{2,1,0:T(4,128)(2,1)} %bitcast.4), calls=%async_computation.1 | async-start | bytes 65536 | tf_op jit(solution)/shard_map/all_to_all | solution.py:116
  34.7 0.1 copy.63
  34.8 8.6 %all-to-all-done.1 = bf16[32,4,128]{2,1,0:T(4,128)(2,1)S(1)} async-done(((bf16[32,4,128]{2,1,0:T(4,128)(2,1)}), bf16[32,4,128]{2,1,0:T(4,128)(2,1)S(1)}, u32[]{:S(2)}, u32[]{:S(2)}) %all-to-all-start.1) | async-done | bytes 32800 | tf_op jit(solution)/shard_map/all_to_all | solution.py:116
  43.4 0.6 copy.60
  44.0 6.3 %all-to-all-start.2 = ((bf16[4,4,1024]{2,1,0:T(4,128)(2,1)}), bf16[4,4,1024]{2,1,0:T(4,128)(2,1)S(1)}, u32[]{:S(2)}, u32[]{:S(2)}) async-start(bf16[4,4,1024]{2,1,0:T(4,128)(2,1)} %copy.60), calls=%async_computation.2 | async-start | bytes 65536 | tf_op jit(solution)/shard_map/all_to_all | solution.py:37
  50.3 0.1 fusion.26
  50.4 3.1 %all-to-all-done.2 = bf16[4,4,1024]{2,1,0:T(4,128)(2,1)S(1)} async-done(((bf16[4,4,1024]{2,1,0:T(4,128)(2,1)}), bf16[4,4,1024]{2,1,0:T(4,128)(2,1)S(1)}, u32[]{:S(2)}, u32[]{:S(2)}) %all-to-all-start.2) | async-done | bytes 32800 | tf_op jit(solution)/shard_map/all_to_all | solution.py:37
  53.5 0.0 copy-done.1
  53.5 0.0 copy-done.2
  53.6 6.0 %all_gather.3 = f32[4096,5]{0,1:T(8,128)S(1)} all-gather(f32[1024,5]{0,1:T(8,128)S(1)} %pad_maximum_fusion), channel_id=1, replica_groups=mesh['dp'=32,'head'=4] {'head'}, dimensions={0}, use_global_device_ids=true | all-gather | bytes 102400 | tf_op jit(solution)/shard_map/all_gather | solution.py:45
  59.6 0.1 multiply_reduce_fusion
  59.8 0.3 convolution_convert_fusion.1
  60.0 0.1 broadcast_in_dim.66
  60.1 0.5 broadcast_in_dim.67
  60.6 14.7 %all_to_all.41 = bf16[32,2,4096]{2,1,0:T(2,128)(2,1)S(1)} all-to-all(bf16[32,2,4096]{2,1,0:T(2,128)(2,1)S(1)} %bitcast.55), channel_id=1, replica_groups=mesh['dp'=32,'head'=4] {'dp'}, dimensions={0} | all-to-all | bytes 1048576 | tf_op jit(solution)/shard_map/all_to_all | solution.py:145
  75.4 0.2 reshape.121
  75.6 3.2 %fusion.3 = f32[64,448]{1,0:T(8,128)S(1)} fusion(bf16[64,4096]{1,0:T(8,128)(2,1)S(1)} %reshape.121, bf16[1,2,4096,448]{2,3,1,0:T(8,128)(2,1)} %param.26), kind=kOutput, calls=%fused_computation.5 | convolution fusion | flops 234881024 | bytes 4308992 | tf_op jit(solution)/shard_map/dot_general | solution.py:148
  78.8 3.2 %fusion.10 = bf16[64,448]{1,0:T(8,128)(2,1)S(1)} fusion(bf16[64,4096]{1,0:T(8,128)(2,1)S(1)} %reshape.121, bf16[1,2,4096,448]{2,3,1,0:T(8,128)(2,1)} %param.26, f32[64,448]{1,0:T(8,128)S(1)} %fusion.3), kind=kOutput, calls=%fused_computation.11 | convolution fusion | flops 235053056 | bytes 4366336 | tf_op jit(solution)/shard_map/dot_general | solution.py:149
  82.0 0.0 copy-start.5
  82.0 2.8 %convolution_convert_fusion = bf16[32,2,4096]{2,0,1:T(8,128)(2,1)S(1)} fusion(bf16[1,448,4096]{2,1,0:T(8,128)(2,1)} %param.27, bf16[32,2,448]{2,1,0:T(2,128)(2,1)S(1)} %dot_general.36), kind=kOutput, calls=%fused_computation | convolution fusion | flops 235143168 | bytes 4251648 | tf_op jit(solution)/shard_map/dot_general | solution.py:151
  84.9 12.5 %all_to_all.42 = bf16[4,32,2,1024]{3,1,2,0:T(8,128)(2,1)S(1)} all-to-all(bf16[4,32,2,1024]{3,1,2,0:T(8,128)(2,1)S(1)} %bitcast.56), channel_id=1, replica_groups=mesh['dp'=32,'head'=4] {'head'}, dimensions={0} | all-to-all | bytes 1048576 | tf_op jit(solution)/shard_map/all_to_all | solution.py:37
  97.3 0.1 reduce_sum.74
  97.4 0.8 copy.67
  98.2 3.9 %all-to-all-start.5 = ((bf16[32,2,1024]{2,1,0:T(2,128)(2,1)}), bf16[32,2,1024]{2,1,0:T(2,128)(2,1)S(1)}, u32[]{:S(2)}, u32[]{:S(2)}) async-start(bf16[32,2,1024]{2,1,0:T(2,128)(2,1)} %copy.67), calls=%async_computation.5 | async-start | bytes 262144 | tf_op jit(solution)/shard_map/all_to_all | solution.py:155
  102.1 0.0 copy-done.5
  102.2 0.1 select_reduce_fusion.1
  102.2 8.8 %all-to-all-done.5 = bf16[32,2,1024]{2,1,0:T(2,128)(2,1)S(1)} async-done(((bf16[32,2,1024]{2,1,0:T(2,128)(2,1)}), bf16[32,2,1024]{2,1,0:T(2,128)(2,1)S(1)}, u32[]{:S(2)}, u32[]{:S(2)}) %all-to-all-start.5) | async-done | bytes 131104 | tf_op jit(solution)/shard_map/all_to_all | solution.py:155
  111.0 0.1 convert_reduce_fusion
  111.2 0.8 fusion.13
  (20 shorter events, 0.4 us)
Async XLA Ops:
  0.0 29.7 %copy-start = (bf16[1024,128]{1,0:T(8,128)(2,1)S(1)}, bf16[1024,128]{1,0:T(8,128)(2,1)}, u32[]{:S(2)}) copy-start(bf16[1024,128]{1,0:T(8,128)(2,1)} %param.22) | copy-start | bytes 786436
  0.0 7.3 %copy-start.3 = (bf16[4,2,128]{2,1,0:T(2,128)(2,1)S(1)}, bf16[4,2,128]{2,1,0:T(2,128)(2,1)}, u32[]{:S(2)}) copy-start(bf16[4,2,128]{2,1,0:T(2,128)(2,1)} %param.17) | copy-start | bytes 6148
  1.4 5.9 %copy-start.6 = (bf16[4,2,2048,128]{3,2,1,0:T(8,128)(2,1)S(1)}, bf16[4,2,2048,128]{3,2,1,0:T(8,128)(2,1)}, u32[]{:S(2)}) copy-start(bf16[4,2,2048,128]{3,2,1,0:T(8,128)(2,1)} %param.19) | copy-start | bytes 12582916
  3.5 16.7 %copy-start.4 = (s32[4,2]{0,1:T(2,128)S(1)}, s32[4,2]{0,1:T(2,128)}, u32[]{:S(2)}) copy-start(s32[4,2]{0,1:T(2,128)} %param.24) | copy-start | bytes 100
  7.0 46.5 %copy-start.1 = (bf16[4,1024]{1,0:T(4,128)(2,1)S(1)}, bf16[4,1024]{1,0:T(4,128)(2,1)}, u32[]{:S(2)}) copy-start(bf16[4,1024]{1,0:T(4,128)(2,1)} %param.14) | copy-start | bytes 24580
  7.0 46.5 %copy-start.2 = (f32[1024]{0:T(1024)S(1)}, f32[1024]{0:T(1024)}, u32[]{:S(2)}) copy-start(f32[1024]{0:T(1024)} %param.23) | copy-start | bytes 12292
  8.9 20.8 %all-to-all-start = ((bf16[32,4,1024]{2,1,0:T(4,128)(2,1)}), bf16[32,4,1024]{2,1,0:T(4,128)(2,1)S(1)}, u32[]{:S(2)}, u32[]{:S(2)}) async-start(bf16[32,4,1024]{2,1,0:T(4,128)(2,1)} %broadcast_in_dim.63), calls=%async_computation | async-start | bytes 524288 | tf_op jit(solution)/shard_map/all_to_all | solution.py:23
  30.6 12.8 %all-to-all-start.1 = ((bf16[32,4,128]{2,1,0:T(4,128)(2,1)}), bf16[32,4,128]{2,1,0:T(4,128)(2,1)S(1)}, u32[]{:S(2)}, u32[]{:S(2)}) async-start(bf16[32,4,128]{2,1,0:T(4,128)(2,1)} %bitcast.4), calls=%async_computation.1 | async-start | bytes 65536 | tf_op jit(solution)/shard_map/all_to_all | solution.py:116
  44.0 9.5 %all-to-all-start.2 = ((bf16[4,4,1024]{2,1,0:T(4,128)(2,1)}), bf16[4,4,1024]{2,1,0:T(4,128)(2,1)S(1)}, u32[]{:S(2)}, u32[]{:S(2)}) async-start(bf16[4,4,1024]{2,1,0:T(4,128)(2,1)} %copy.60), calls=%async_computation.2 | async-start | bytes 65536 | tf_op jit(solution)/shard_map/all_to_all | solution.py:37
  82.0 20.2 %copy-start.5 = (f32[4,2]{0,1:T(2,128)S(1)}, f32[4,2]{0,1:T(2,128)}, u32[]{:S(2)}) copy-start(f32[4,2]{0,1:T(2,128)} %param.25) | copy-start | bytes 100
  98.2 12.8 %all-to-all-start.5 = ((bf16[32,2,1024]{2,1,0:T(2,128)(2,1)}), bf16[32,2,1024]{2,1,0:T(2,128)(2,1)S(1)}, u32[]{:S(2)}, u32[]{:S(2)}) async-start(bf16[32,2,1024]{2,1,0:T(2,128)(2,1)} %copy.67), calls=%async_computation.5 | async-start | bytes 262144 | tf_op jit(solution)/shard_map/all_to_all | solution.py:155
where the time goes:
time: 114 us; the launch traced here: 112 us
  blocking collectives  33.2 us (29%)
  waiting for transfers between devices  29.3 us (26%)
  starting transfers between devices  25.7 us (23%)
  matrix products  16.4 us (14%)
  local copies, waits for them, and re-layouts  4.12 us (4%)
  other arithmetic  2.97 us (3%)
    all_to_all x1, blocking collectives, shards(): lax.all_to_all(outgoing, 'dp', split_axis=0, concat_axis=0, tiled=True)  14.7 us
    all_to_all x1, blocking collectives, sent_and_summed(): lax.all_to_all(parts, axis, split_axis=0, concat_axis=0, tiled=True)  12.5 us
    all_to_all x1, starting transfers between devices, copy_for_each(): return lax.all_to_all(copies, axis, split_axis=0, concat_axis=0, tiled=True)  11.3 us
    all_to_all x1, waiting for transfers between devices, copy_for_each(): return lax.all_to_all(copies, axis, split_axis=0, concat_axis=0, tiled=True)  8.85 us
    all_to_all x1, waiting for transfers between devices, shards(): lax.all_to_all(summed_total.astype(jnp.bfloat16), 'dp', split_axis=0, con...  8.81 us
    all_to_all x1, waiting for transfers between devices, shards(): lax.all_to_all(column_part.astype(jnp.bfloat16), 'dp', split_axis=0, conc...  8.56 us
    all_to_all x1, starting transfers between devices, sent_and_summed(): lax.all_to_all(parts, axis, split_axis=0, concat_axis=0, tiled=True)  6.28 us
    all_gather x1, blocking collectives, rows_first(): whole = lax.all_gather(both, axis, axis=0, tiled=True)  6.03 us
  transfers between devices with their start and end apart: 4, of which 4 were waited for; matrix products, arithmetic and copies ran while one was open for 1% of the time, Pallas kernels for 0%

commit v1 on v0

v1 whole, which is shorter than its diff:
```python
import functools

import jax
import jax.numpy as jnp
from jax import lax
from jax.experimental import pallas as pl
from jax.experimental.pallas import tpu as pltpu
from jax.sharding import PartitionSpec as P

EXPERTS = 8
PAGE = 16
EPSILON = 1e-05
F32 = jnp.float32
BF16 = jnp.bfloat16
I32 = jnp.int32
MESH = pl.DeviceIdType.MESH


def whole_wait(ref, sem):
    pltpu.make_async_copy(ref, ref, sem).wait()


def layer(
    ids_ref,
    gates_ref,
    len_ref,
    residual_ref,
    query_ref,
    fresh_ref,
    vnew_ref,
    pages_ref,
    gain_ref,
    key_hbm,
    value_hbm,
    wout_hbm,
    win_hbm,
    wdown_hbm,
    out_ref,
    key_buf,
    value_buf,
    wout_buf,
    win_buf,
    wdown_buf,
    attn_buf,
    recv_a,
    rows_f,
    msg_buf,
    recv_m,
    recv_g,
    part_buf,
    recv_r,
    stream_buf,
    sel_buf,
    recv_b,
    recv_s,
    x_buf,
    slab_f,
    slab_b,
    recv_c,
    mix_f,
    kv_sem,
    w_sem,
    send_sem,
    recv_sem,
):
    d = lax.axis_index("dp")
    h = lax.axis_index("head")
    me = d * 4 + h

    def device(index):
        return (index // 4, lax.rem(index, 4))

    for b in range(4):
        pltpu.make_async_copy(key_hbm.at[b], key_buf.at[b], kv_sem.at[0, b]).start()
        pltpu.make_async_copy(value_hbm.at[b], value_buf.at[b], kv_sem.at[1, b]).start()
    pltpu.make_async_copy(wout_hbm, wout_buf, w_sem.at[0]).start()
    pltpu.make_async_copy(win_hbm.at[0], win_buf, w_sem.at[1]).start()
    pltpu.make_async_copy(wdown_hbm.at[0], wdown_buf, w_sem.at[2]).start()

    barrier = pltpu.get_barrier_semaphore()

    def greet(i, carry):
        pl.semaphore_signal(
            barrier, inc=1, device_id=device(lax.rem(me + i, 128)), device_id_type=MESH
        )
        return carry

    lax.fori_loop(1, 128, greet, 0)

    ids = [ids_ref[t, j] for t in range(4) for j in range(2)]
    slots = []
    for a in range(8):
        earlier = jnp.int32(0)
        for c in range(a):
            earlier = earlier + (ids[c] == ids[a]).astype(I32)
        slots.append(earlier)
    block = lax.rem(d, 8)

    lane = lax.broadcasted_iota(I32, (8, 128), 1)
    row8 = lax.broadcasted_iota(I32, (8, 128), 0)
    target = jnp.zeros((8, 128), I32)
    for t in range(4):
        for j in range(2):
            a = t * 2 + j
            value = ids[a] * 16 + block * 2 + slots[a]
            target = jnp.where((row8 == 4 + j) & (lane == block * 4 + t), value, target)
    target = target.astype(F32)
    for j in range(8):
        res = residual_ref[:, j * 128 : (j + 1) * 128].astype(F32)
        both = jnp.concatenate([res, jnp.zeros((4, 128), F32)], axis=0)
        msg_buf[j] = (both + target).astype(BF16)

    head_lane = lax.broadcasted_iota(I32, (128, 128), 1)
    page_row = lax.broadcasted_iota(I32, (128, 64), 0)
    chosen = jnp.zeros((128, 128), F32)
    for b in range(4):
        for k in range(2):
            hit = (pages_ref[b, k : k + 1, :] == page_row).astype(F32)
            column = jnp.sum(hit, axis=1, keepdims=True)
            chosen = jnp.where((head_lane >> 2) == b * 2 + k, column, chosen)
    chosen_rows = chosen.T[:32, :].astype(BF16)
    spread = (
        (lax.broadcasted_iota(I32, (128, 2048), 1) >> 4)
        == lax.broadcasted_iota(I32, (128, 2048), 0)
    ).astype(F32).astype(BF16)
    mask = jnp.dot(chosen_rows, spread, preferred_element_type=F32)

    position = lax.broadcasted_iota(I32, (8, 2048), 1)
    top_rows = lax.broadcasted_iota(I32, (8, 1), 0) < 4
    scale = 128.0 ** (-0.5)
    nt = (((1,), (1,)), ((), ()))
    for b in range(4):
        q = query_ref[b]
        qf = q.astype(F32)
        fresh = jnp.where(
            top_rows, fresh_ref[b, 0:1, :].astype(F32), fresh_ref[b, 1:2, :].astype(F32)
        )
        own = jnp.sum(qf * fresh, axis=1, keepdims=True) * scale
        live = (mask[b * 8 : (b + 1) * 8] > 0.5) & (position < len_ref[b])
        pltpu.make_async_copy(key_hbm.at[b], key_buf.at[b], kv_sem.at[0, b]).wait()
        s0 = lax.dot_general(q, key_buf[b, 0], nt, preferred_element_type=F32)
        s1 = lax.dot_general(q, key_buf[b, 1], nt, preferred_element_type=F32)
        scores = jnp.where(top_rows, s0, s1) * scale
        masked = jnp.where(live, scores, -1e30)
        top = jnp.maximum(jnp.max(masked, axis=1, keepdims=True), own)
        expo = jnp.where(live, jnp.exp(scores - top), 0.0)
        own_expo = jnp.exp(own - top)
        total = jnp.sum(expo, axis=1, keepdims=True) + own_expo
        weights = (expo / total).astype(BF16)
        own_weight = (own_expo / total).astype(BF16).astype(F32)
        pltpu.make_async_copy(value_hbm.at[b], value_buf.at[b], kv_sem.at[1, b]).wait()
        a0 = jnp.dot(weights, value_buf[b, 0], preferred_element_type=F32)
        a1 = jnp.dot(weights, value_buf[b, 1], preferred_element_type=F32)
        new = jnp.where(
            top_rows, vnew_ref[b, 0:1, :].astype(F32), vnew_ref[b, 1:2, :].astype(F32)
        )
        attn_buf[b * 8 : (b + 1) * 8, :] = (
            jnp.where(top_rows, a0, a1) + own_weight * new
        ).astype(BF16)

    pl.semaphore_wait(barrier, 127)

    def send_rows(i, carry):
        to = lax.rem(d + i, 32)
        pltpu.make_async_remote_copy(
            attn_buf, recv_a.at[d], send_sem.at[0], recv_sem.at[0], (to, h), MESH
        ).start()
        return carry

    lax.fori_loop(1, 32, send_rows, 0)
    pltpu.make_async_copy(attn_buf, recv_a.at[d], recv_sem.at[0]).start()

    quarter = d // 8

    def send_message(j, carry):
        to = h * 8 + j
        here = (to == d) & (quarter == h)

        @pl.when(here)
        def _():
            pltpu.make_async_copy(msg_buf.at[j], recv_m.at[block], recv_sem.at[1]).start()

        @pl.when(jnp.logical_not(here))
        def _():
            pltpu.make_async_remote_copy(
                msg_buf.at[j],
                recv_m.at[block],
                send_sem.at[1],
                recv_sem.at[1],
                (to, quarter),
                MESH,
            ).start()

        return carry

    lax.fori_loop(0, 8, send_message, 0)
    for i in range(1, 4):
        pltpu.make_async_remote_copy(
            gain_ref, recv_g.at[h], send_sem.at[2], recv_sem.at[2], (d, lax.rem(h + i, 4)), MESH
        ).start()
    pltpu.make_async_copy(gain_ref, recv_g.at[h], recv_sem.at[2]).start()

    whole_wait(recv_m, recv_sem.at[1])
    messages = recv_m[...].astype(F32).reshape(64, 128).astype(BF16)
    pick_row = lax.broadcasted_iota(I32, (40, 64), 0)
    pick_col = lax.broadcasted_iota(I32, (40, 64), 1)
    pick = (
        ((pick_row < 32) & (pick_col == (pick_row >> 2) * 8 + (pick_row & 3)))
        | ((pick_row == 32) & ((pick_col & 7) == 4))
        | ((pick_row == 33) & ((pick_col & 7) == 5))
    )
    picked = jnp.dot(pick.astype(F32).astype(BF16), messages, preferred_element_type=F32)
    residual = picked[:32]
    slot_row = lax.broadcasted_iota(I32, (128, 128), 0).astype(F32)
    select = ((slot_row == picked[32:33]) | (slot_row == picked[33:34])).astype(F32)
    select = select[:, :32].astype(BF16)
    pltpu.make_async_copy(wout_hbm, wout_buf, w_sem.at[0]).wait()

    whole_wait(recv_a, recv_sem.at[0])
    rows_f[...] = recv_a[...].astype(F32).reshape(1024, 128)
    columns = jnp.zeros((128, 128), F32)
    for n in range(4):
        pair = jnp.concatenate(
            [rows_f[pl.ds(n * 2 + m, 128, stride=8), :] for m in range(2)], axis=1
        ).astype(BF16)
        columns = columns + jnp.dot(
            pair, wout_buf[n * 256 : (n + 1) * 256, :], preferred_element_type=F32
        )
    part_buf[...] = columns.astype(BF16).reshape(4, 32, 128)

    for i in range(1, 4):
        to = lax.rem(h + i, 4)
        pltpu.make_async_remote_copy(
            part_buf.at[to], recv_r.at[h], send_sem.at[3], recv_sem.at[3], (d, to), MESH
        ).start()
    pltpu.make_async_copy(part_buf.at[h], recv_r.at[h], recv_sem.at[3]).start()
    whole_wait(recv_r, recv_sem.at[3])
    stream = residual
    for i in range(4):
        stream = stream + recv_r[i].astype(F32)
    stream_buf[...] = stream.reshape(4, 8, 128)
    sel_buf[...] = (
        jnp.dot(select, stream.astype(BF16), preferred_element_type=F32)
        .astype(BF16)
        .reshape(8, 16, 128)
    )

    def send_slots(i, carry):
        to = lax.rem(me + i, 128)
        pltpu.make_async_remote_copy(
            sel_buf.at[to // 16],
            recv_b.at[me],
            send_sem.at[4],
            recv_sem.at[4],
            device(to),
            MESH,
        ).start()
        return carry

    lax.fori_loop(1, 128, send_slots, 0)
    pltpu.make_async_copy(sel_buf.at[me // 16], recv_b.at[me], recv_sem.at[4]).start()

    def send_stream(b, carry):
        to = h * 8 + b
        here = (to == d) & (quarter == h)

        @pl.when(here)
        def _():
            pltpu.make_async_copy(
                stream_buf.at[b // 2], recv_s.at[block], recv_sem.at[5]
            ).start()

        @pl.when(jnp.logical_not(here))
        def _():
            pltpu.make_async_remote_copy(
                stream_buf.at[b // 2],
                recv_s.at[block],
                send_sem.at[5],
                recv_sem.at[5],
                (to, quarter),
                MESH,
            ).start()

        return carry

    lax.fori_loop(0, 8, send_stream, 0)

    pltpu.make_async_copy(win_hbm.at[0], win_buf, w_sem.at[1]).wait()
    pltpu.make_async_copy(wdown_hbm.at[0], wdown_buf, w_sem.at[2]).wait()
    whole_wait(recv_g, recv_sem.at[2])
    whole_wait(recv_b, recv_sem.at[4])
    squares = jnp.zeros((64, 128), F32)
    for n in range(32):
        x = recv_b[n * 4 : (n + 1) * 4].reshape(64, 128).astype(F32)
        squares = squares + x * x
        x_buf[:, n * 128 : (n + 1) * 128] = (
            x * recv_g[n // 8, n % 8 : n % 8 + 1, :]
        ).astype(BF16)
    inverse = lax.rsqrt(jnp.sum(squares, axis=1, keepdims=True) * (1.0 / 4096.0) + EPSILON)
    gate = jnp.dot(x_buf[...], win_buf[0], preferred_element_type=F32) * inverse
    up = jnp.dot(x_buf[...], win_buf[1], preferred_element_type=F32) * inverse
    hidden = (gate * jax.nn.sigmoid(gate) * up).astype(BF16)
    for n in range(16):
        slab = jnp.dot(
            hidden, wdown_buf[:, n * 256 : (n + 1) * 256], preferred_element_type=F32
        )
        for m in range(2):
            j = (n * 2 + m) % 8
            slab_f[n // 4, pl.ds(j, 64, stride=8), :] = slab[:, m * 128 : (m + 1) * 128]
    slab_b[...] = slab_f[...].astype(BF16).reshape(4, 32, 16, 128)

    def send_back(i, carry):
        to = lax.rem(me + i, 128)
        pltpu.make_async_remote_copy(
            slab_b.at[lax.rem(to, 4), to // 4],
            recv_c.at[me],
            send_sem.at[6],
            recv_sem.at[6],
            device(to),
            MESH,
        ).start()
        return carry

    lax.fori_loop(1, 128, send_back, 0)
    pltpu.make_async_copy(slab_b.at[h, d], recv_c.at[me], recv_sem.at[6]).start()

    slot16 = lax.broadcasted_iota(I32, (16, 128), 0)
    factors = []
    for t in range(4):
        factor = jnp.zeros((16, 128), F32)
        for j in range(2):
            a = t * 2 + j
            factor = factor + jnp.where(slot16 == ids[a] * 2 + slots[a], gates_ref[t, j], 0.0)
        factors.append(factor)
    odd = lax.rem(d, 2) == 1

    whole_wait(recv_s, recv_sem.at[5])
    whole_wait(recv_c, recv_sem.at[6])
    for e in range(8):
        total = recv_c[e * 16].astype(F32)
        for i in range(1, 16):
            total = total + recv_c[e * 16 + i].astype(F32)
        mix_f[e * 16 : (e + 1) * 16, :] = total
    for j in range(8):
        slot_rows = mix_f[pl.ds(j, 16, stride=8), :]
        mixed = jnp.concatenate(
            [jnp.sum(slot_rows * f, axis=0, keepdims=True) for f in factors], axis=0
        )
        own_stream = recv_s[j]
        own_stream = jnp.where(odd, own_stream[4:], own_stream[:4])
        out_ref[:, j * 128 : (j + 1) * 128] = (own_stream + mixed).astype(BF16)

    whole_wait(recv_a.at[pl.ds(0, 31)], send_sem.at[0])
    apart = (quarter != h).astype(I32)

    @pl.when(quarter == h)
    def _():
        whole_wait(recv_m.at[pl.ds(0, 7)], send_sem.at[1])
        whole_wait(recv_s.at[pl.ds(0, 7)], send_sem.at[5])

    @pl.when(quarter != h)
    def _():
        whole_wait(recv_m, send_sem.at[1])
        whole_wait(recv_s, send_sem.at[5])

    whole_wait(recv_g.at[pl.ds(0, 3)], send_sem.at[2])
    whole_wait(recv_r.at[pl.ds(0, 3)], send_sem.at[3])
    whole_wait(recv_b.at[pl.ds(0, 127)], send_sem.at[4])
    whole_wait(recv_c.at[pl.ds(0, 127)], send_sem.at[6])


def shards(
    residual,
    query,
    fresh_token_keys,
    value_new,
    key_cache,
    value_cache,
    lengths,
    pages,
    w_out,
    norm_gain,
    expert_ids,
    gate_weights,
    w_in,
    w_down,
):
    smem = pl.BlockSpec(memory_space=pltpu.SMEM)
    vmem = pl.BlockSpec(memory_space=pltpu.VMEM)
    hbm = pl.BlockSpec(memory_space=pltpu.HBM)
    return pl.pallas_call(
        layer,
        out_shape=jax.ShapeDtypeStruct((4, 1024), BF16),
        in_specs=[smem] * 3 + [vmem] * 6 + [hbm] * 5,
        out_specs=vmem,
        scratch_shapes=[
            pltpu.VMEM((4, 2, 2048, 128), BF16),
            pltpu.VMEM((4, 2, 2048, 128), BF16),
            pltpu.VMEM((1024, 128), BF16),
            pltpu.VMEM((2, 4096, 448), BF16),
            pltpu.VMEM((448, 4096), BF16),
            pltpu.VMEM((32, 128), BF16),
            pltpu.VMEM((32, 32, 128), BF16),
            pltpu.VMEM((1024, 128), F32),
            pltpu.VMEM((8, 8, 128), BF16),
            pltpu.VMEM((8, 8, 128), BF16),
            pltpu.VMEM((4, 8, 128), F32),
            pltpu.VMEM((4, 32, 128), BF16),
            pltpu.VMEM((4, 32, 128), BF16),
            pltpu.VMEM((4, 8, 128), F32),
            pltpu.VMEM((8, 16, 128), BF16),
            pltpu.VMEM((128, 16, 128), BF16),
            pltpu.VMEM((8, 8, 128), F32),
            pltpu.VMEM((64, 4096), BF16),
            pltpu.VMEM((4, 512, 128), F32),
            pltpu.VMEM((4, 32, 16, 128), BF16),
            pltpu.VMEM((128, 16, 128), BF16),
            pltpu.VMEM((128, 128), F32),
            pltpu.SemaphoreType.DMA((2, 4)),
            pltpu.SemaphoreType.DMA((3,)),
            pltpu.SemaphoreType.DMA((7,)),
            pltpu.SemaphoreType.DMA((7,)),
        ],
        compiler_params=pltpu.CompilerParams(
            collective_id=0, has_side_effects=True, vmem_limit_bytes=60 * 1024 * 1024
        ),
        name="layer",
    )(
        expert_ids,
        gate_weights,
        lengths,
        residual,
        query,
        fresh_token_keys,
        value_new,
        pages,
        norm_gain.reshape(8, 128),
        key_cache,
        value_cache,
        w_out,
        w_in,
        w_down,
    )


def solution(mesh):
    in_specs = (
        P("dp", "head"),
        P("dp", "head", None),
        P("dp", "head", None),
        P("dp", "head", None),
        P("dp", "head", None, None),
        P("dp", "head", None, None),
        P("dp"),
        P("dp", "head", None),
        P("head", "dp"),
        P("head"),
        P("dp", None),
        P("dp", None),
        P("dp", None, None, "head"),
        P("dp", "head", None),
    )
    out_specs = P("dp", "head")
    return jax.shard_map(shards, mesh=mesh, in_specs=in_specs, out_specs=out_specs, check_vma=False)
```

time: 114 us -> 63.3 us (0.56); the launches traced: 112 us -> 62.8 us
  Pallas kernels: 0 us -> 47.2 us
  blocking collectives: 33.2 us -> 0 us
  waiting for transfers between devices: 29.3 us -> 0 us
  starting transfers between devices: 25.7 us -> 0 us
  matrix products: 16.4 us -> 0 us
  local copies, waits for them, and re-layouts: 4.12 us -> 15.5 us
  other arithmetic: 2.97 us -> 0 us
    pallas_call x0 -> x1, Pallas kernels: none -> 47.2 us  [shards(): pl.pallas_call(layer, out_shape=jax.ShapeDtypeStruct((4, 1024), BF16), in...]
    all_to_all x4 -> x0, waiting for transfers between devices: 29.3 us -> none  [the longest x1 8.85 us: copy_for_each(): return lax.all_to_all(copies, axis, split_axis=0, concat_axis=0, tiled=True)]
    all_to_all x2 -> x0, blocking collectives: 27.2 us -> none  [the longest x1 14.7 us: shards(): lax.all_to_all(outgoing, 'dp', split_axis=0, concat_axis=0, tiled=True)]
    all_to_all x4 -> x0, starting transfers between devices: 25.7 us -> none  [the longest x1 11.3 us: copy_for_each(): return lax.all_to_all(copies, axis, split_axis=0, concat_axis=0, tiled=True)]
    dot_general x9 -> x0, matrix products: 16.4 us -> none  [the longest x1 3.49 us: shards(): jnp.einsum('bkgd,bksd->bkgs', grouped_rows, key_cache, preferred_element_...]
    unnamed x16 -> x4, local copies, waits for them, and re-layouts: 0.14 us -> 15.5 us
    all_gather x1 -> x0, blocking collectives: 6.03 us -> none  [rows_first(): whole = lax.all_gather(both, axis, axis=0, tiled=True)]
    broadcast_in_dim x4 -> x0, local copies, waits for them, and re-layouts: 1.54 us -> none  [the longest x1 0.77 us: copy_for_each(): copies = jnp.broadcast_to(value, (lax.axis_size(axis), *value.shape))]
  transfers between devices with their start and end apart: 4 -> 0, of which waited for: 4 -> 0; matrix products, arithmetic and copies ran while one was open for 1% -> 0% of each run, Pallas kernels for 0% -> 0%
where the time goes in v1:
time: 63.3 us; the launch traced here: 62.8 us
  Pallas kernels  47.2 us (75%)
  local copies, waits for them, and re-layouts  15.5 us (24%)
    pallas_call x1, Pallas kernels, shards(): pl.pallas_call(layer, out_shape=jax.ShapeDtypeStruct((4, 1024), BF16), in...  47.2 us
    unnamed x4, local copies, waits for them, and re-layouts  15.5 us

profile of v1, /device:TPU:1, one launch (start us, length us, event | category | flops | bytes accessed | tf_op | source)
XLA Modules:
  0.0 62.8 jit_solution(12234839494117327052)
XLA Ops:
  0.0 1.3 %copy.15.ids_ref = s32[4,2]{1,0:T(4,128)} copy(s32[4,2]{0,1:T(2,128)} %param.24) | data formatting | bytes 64 | tf_op args[10]
  1.3 1.3 %copy.16.gates_ref = f32[4,2]{1,0:T(4,128)} copy(f32[4,2]{0,1:T(2,128)} %param.25) | data formatting | bytes 64 | tf_op args[11]
  2.7 11.6 %copy.17.win_hbm = bf16[1,2,4096,448]{3,2,1,0:T(8,128)(2,1)} copy(bf16[1,2,4096,448]{2,3,1,0:T(8,128)(2,1)} %param.26) | data formatting | bytes 14680064 | tf_op args[12]
  14.2 47.2 %layer.1 = bf16[4,1024]{1,0:T(4,128)(2,1)} custom-call(s32[4,2]{1,0:T(4,128)} %copy.15.ids_ref, f32[4,2]{1,0:T(4,128)} %copy.16.gates_ref, s32[4]{0:T(128)} %len_ref.1, bf16[4,1024]{1,0:T(4,128)(2,1)} %residual_ref.1, bf16[4,8,128]{2,1,0:T(8,128)(2,1)} %query_ref.1, bf16[4,2,128]{2,1,0:T(2,128)(2,1)} %fresh_ref.1, bf16[4,2,128]{2,1,0:T(2,128)(2,1)} %vnew_ref.1, ...), custom_call_target="tpu_custom_call" | custom-call | tf_op jit(solution)/shard_map/layer/pallas_call | solution.py:391
  61.5 1.3 %copy.19 = bf16[4,1024]{1,0:T(4,128)(2,1)} copy(bf16[4,1024]{1,0:T(4,128)(2,1)} %layer.1) | data formatting | bytes 16384

commit v2 on v1

--- a/solution.py
+++ b/solution.py
@@ -87,7 +87,7 @@
 
     lax.fori_loop(1, 128, greet, 0)
 
-    ids = [ids_ref[t, j] for t in range(4) for j in range(2)]
+    ids = [ids_ref[j, t] for t in range(4) for j in range(2)]
     slots = []
     for a in range(8):
         earlier = jnp.int32(0)
@@ -297,8 +297,8 @@
             x * recv_g[n // 8, n % 8 : n % 8 + 1, :]
         ).astype(BF16)
     inverse = lax.rsqrt(jnp.sum(squares, axis=1, keepdims=True) * (1.0 / 4096.0) + EPSILON)
-    gate = jnp.dot(x_buf[...], win_buf[0], preferred_element_type=F32) * inverse
-    up = jnp.dot(x_buf[...], win_buf[1], preferred_element_type=F32) * inverse
+    gate = lax.dot_general(x_buf[...], win_buf[0], nt, preferred_element_type=F32) * inverse
+    up = lax.dot_general(x_buf[...], win_buf[1], nt, preferred_element_type=F32) * inverse
     hidden = (gate * jax.nn.sigmoid(gate) * up).astype(BF16)
     for n in range(16):
         slab = jnp.dot(
@@ -330,7 +330,7 @@
         factor = jnp.zeros((16, 128), F32)
         for j in range(2):
             a = t * 2 + j
-            factor = factor + jnp.where(slot16 == ids[a] * 2 + slots[a], gates_ref[t, j], 0.0)
+            factor = factor + jnp.where(slot16 == ids[a] * 2 + slots[a], gates_ref[j, t], 0.0)
         factors.append(factor)
     odd = lax.rem(d, 2) == 1
 
@@ -397,7 +397,7 @@
             pltpu.VMEM((4, 2, 2048, 128), BF16),
             pltpu.VMEM((4, 2, 2048, 128), BF16),
             pltpu.VMEM((1024, 128), BF16),
-            pltpu.VMEM((2, 4096, 448), BF16),
+            pltpu.VMEM((2, 448, 4096), BF16),
             pltpu.VMEM((448, 4096), BF16),
             pltpu.VMEM((32, 128), BF16),
             pltpu.VMEM((32, 32, 128), BF16),
@@ -426,8 +426,8 @@
         ),
         name="layer",
     )(
-        expert_ids,
-        gate_weights,
+        expert_ids.T,
+        gate_weights.T,
         lengths,
         residual,
         query,
@@ -438,7 +438,7 @@
         key_cache,
         value_cache,
         w_out,
-        w_in,
+        jnp.swapaxes(w_in, 2, 3),
         w_down,
     )
 

time: 63.3 us -> 49.4 us (0.78)
  local copies, waits for them, and re-layouts: 15.5 us -> 1.3 us
  Pallas kernels: 47.2 us -> 47.9 us
    unnamed x4 -> x1, local copies, waits for them, and re-layouts: 15.5 us -> 1.3 us
    pallas_call x1, Pallas kernels: 47.2 us -> 47.9 us  [shards(): pl.pallas_call(layer, out_shape=jax.ShapeDtypeStruct((4, 1024), BF16), in...]
where the time goes in v2:
time: 49.4 us; the launch traced here: 49.2 us
  Pallas kernels  47.9 us (97%)
  local copies, waits for them, and re-layouts  1.3 us (3%)
    pallas_call x1, Pallas kernels, shards(): pl.pallas_call(layer, out_shape=jax.ShapeDtypeStruct((4, 1024), BF16), in...  47.9 us
    unnamed x1, local copies, waits for them, and re-layouts  1.3 us

profile of v2, /device:TPU:1, one launch (start us, length us, event | category | flops | bytes accessed | tf_op | source)
XLA Modules:
  0.0 49.2 jit_solution(5830716407706716781)
XLA Ops:
  0.0 47.9 %layer.1 = bf16[4,1024]{1,0:T(4,128)(2,1)} custom-call(s32[2,4]{1,0:T(2,128)} %bitcast.6, f32[2,4]{1,0:T(2,128)} %bitcast.7, s32[4]{0:T(128)} %len_ref.1, bf16[4,1024]{1,0:T(4,128)(2,1)} %residual_ref.1, bf16[4,8,128]{2,1,0:T(8,128)(2,1)} %query_ref.1, bf16[4,2,128]{2,1,0:T(2,128)(2,1)} %fresh_ref.1, bf16[4,2,128]{2,1,0:T(2,128)(2,1)} %vnew_ref.1, ...), custom_call_target="tpu_custom_call" | custom-call | tf_op jit(solution)/shard_map/layer/pallas_call | solution.py:391
  47.9 1.3 %copy.16 = bf16[4,1024]{1,0:T(4,128)(2,1)} copy(bf16[4,1024]{1,0:T(4,128)(2,1)} %layer.1) | data formatting | bytes 16384

commit v3 on v2

--- a/solution.py
+++ b/solution.py
@@ -14,6 +14,9 @@
 BF16 = jnp.bfloat16
 I32 = jnp.int32
 MESH = pl.DeviceIdType.MESH
+FAR = sorted(range(1, 32), key=lambda i: -(2 * (i >> 4) + (0, 1, 2, 1)[i >> 2 & 3] + (0, 1, 2, 1)[i & 3]))
+ORDER = (0, 1, 2, 3)
+OUT_SPACE = pl.ANY
 
 
 def whole_wait(ref, sem):
@@ -21,6 +24,21 @@
 
 
 def layer(
+    ids_hbm,
+    gates_hbm,
+    len_hbm,
+    residual_hbm,
+    query_hbm,
+    fresh_hbm,
+    vnew_hbm,
+    pages_hbm,
+    gain_hbm,
+    key_hbm,
+    value_hbm,
+    wout_hbm,
+    win_hbm,
+    wdown_hbm,
+    out_hbm,
     ids_ref,
     gates_ref,
     len_ref,
@@ -30,11 +48,6 @@
     vnew_ref,
     pages_ref,
     gain_ref,
-    key_hbm,
-    value_hbm,
-    wout_hbm,
-    win_hbm,
-    wdown_hbm,
     out_ref,
     key_buf,
     value_buf,
@@ -55,47 +68,73 @@
     recv_s,
     x_buf,
     slab_f,
+    sib_buf,
+    recv_d,
     slab_b,
     recv_c,
     mix_f,
+    in_sem,
     kv_sem,
     w_sem,
     send_sem,
     recv_sem,
+    group_sem,
+    pass_send,
+    pass_recv,
+    sib_send,
+    sib_recv,
 ):
     d = lax.axis_index("dp")
     h = lax.axis_index("head")
-    me = d * 4 + h
-
-    def device(index):
-        return (index // 4, lax.rem(index, 4))
+    y = h >> 1
+    c = h & 1
+    sibling = (d, h ^ 1)
+    quarter = d >> 3
+    block = d & 7
+
+    barrier = pltpu.get_barrier_semaphore()
+
+    def greet(to):
+        pl.semaphore_signal(barrier, inc=1, device_id=to, device_id_type=MESH)
+
+    small = [
+        (ids_hbm, ids_ref),
+        (gates_hbm, gates_ref),
+        (len_hbm, len_ref),
+        (pages_hbm, pages_ref),
+        (query_hbm, query_ref),
+        (fresh_hbm, fresh_ref),
+        (residual_hbm, residual_ref),
+        (vnew_hbm, vnew_ref),
+        (gain_hbm, gain_ref),
+    ]
+    for n, (source, target) in enumerate(small):
+        pltpu.make_async_copy(source, target, in_sem.at[n]).start()
+
+    for i in FAR:
+        for side in range(2):
+            greet((d ^ i, side * 2 + c))
+    for i in range(1, 4):
+        greet((d, h ^ i))
+    for j in range(8):
+
+        @pl.when(jnp.logical_not((h * 8 + j == d) & (quarter == h)))
+        def _():
+            greet((h * 8 + j, quarter))
 
     for b in range(4):
         pltpu.make_async_copy(key_hbm.at[b], key_buf.at[b], kv_sem.at[0, b]).start()
         pltpu.make_async_copy(value_hbm.at[b], value_buf.at[b], kv_sem.at[1, b]).start()
-    pltpu.make_async_copy(wout_hbm, wout_buf, w_sem.at[0]).start()
-    pltpu.make_async_copy(win_hbm.at[0], win_buf, w_sem.at[1]).start()
-    pltpu.make_async_copy(wdown_hbm.at[0], wdown_buf, w_sem.at[2]).start()
-
-    barrier = pltpu.get_barrier_semaphore()
-
-    def greet(i, carry):
-        pl.semaphore_signal(
-            barrier, inc=1, device_id=device(lax.rem(me + i, 128)), device_id_type=MESH
-        )
-        return carry
-
-    lax.fori_loop(1, 128, greet, 0)
+    for n, (source, target) in enumerate(small):
+        pltpu.make_async_copy(source, target, in_sem.at[n]).wait()
 
     ids = [ids_ref[j, t] for t in range(4) for j in range(2)]
     slots = []
     for a in range(8):
         earlier = jnp.int32(0)
-        for c in range(a):
-            earlier = earlier + (ids[c] == ids[a]).astype(I32)
+        for n in range(a):
+            earlier = earlier + (ids[n] == ids[a]).astype(I32)
         slots.append(earlier)
-    block = lax.rem(d, 8)
-
     lane = lax.broadcasted_iota(I32, (8, 128), 1)
     row8 = lax.broadcasted_iota(I32, (8, 128), 0)
     target = jnp.zeros((8, 128), I32)
@@ -158,47 +197,41 @@
             jnp.where(top_rows, a0, a1) + own_weight * new
         ).astype(BF16)
 
-    pl.semaphore_wait(barrier, 127)
-
-    def send_rows(i, carry):
-        to = lax.rem(d + i, 32)
-        pltpu.make_async_remote_copy(
-            attn_buf, recv_a.at[d], send_sem.at[0], recv_sem.at[0], (to, h), MESH
-        ).start()
-        return carry
-
-    lax.fori_loop(1, 32, send_rows, 0)
-    pltpu.make_async_copy(attn_buf, recv_a.at[d], recv_sem.at[0]).start()
-
-    quarter = d // 8
-
-    def send_message(j, carry):
-        to = h * 8 + j
-        here = (to == d) & (quarter == h)
-
-        @pl.when(here)
+    pltpu.make_async_copy(wout_hbm, wout_buf, w_sem.at[0]).start()
+    pltpu.make_async_copy(win_hbm.at[0], win_buf, w_sem.at[1]).start()
+    pltpu.make_async_copy(wdown_hbm.at[0], wdown_buf, w_sem.at[2]).start()
+    here = quarter == h
+    pl.semaphore_wait(barrier, 73 - here.astype(I32))
+    for j in range(8):
+        own_place = here & (h * 8 + j == d)
+
+        @pl.when(own_place)
         def _():
             pltpu.make_async_copy(msg_buf.at[j], recv_m.at[block], recv_sem.at[1]).start()
 
-        @pl.when(jnp.logical_not(here))
+        @pl.when(jnp.logical_not(own_place))
         def _():
             pltpu.make_async_remote_copy(
                 msg_buf.at[j],
                 recv_m.at[block],
                 send_sem.at[1],
                 recv_sem.at[1],
-                (to, quarter),
+                (h * 8 + j, quarter),
                 MESH,
             ).start()
 
-        return carry
-
-    lax.fori_loop(0, 8, send_message, 0)
+    for i in FAR:
+        pltpu.make_async_remote_copy(
+            attn_buf, recv_a.at[d], send_sem.at[0], recv_sem.at[0], (d ^ i, h), MESH
+        ).start()
+    pltpu.make_async_copy(attn_buf, recv_a.at[d], recv_sem.at[0]).start()
+
+    own_gains = recv_g.at[pl.ds(pl.multiple_of(h * 8, 8), 8)]
     for i in range(1, 4):
         pltpu.make_async_remote_copy(
-            gain_ref, recv_g.at[h], send_sem.at[2], recv_sem.at[2], (d, lax.rem(h + i, 4)), MESH
+            gain_ref, own_gains, send_sem.at[2], recv_sem.at[2], (d, h ^ i), MESH
         ).start()
-    pltpu.make_async_copy(gain_ref, recv_g.at[h], recv_sem.at[2]).start()
+    pltpu.make_async_copy(gain_ref, own_gains, recv_sem.at[2]).start()
 
     whole_wait(recv_m, recv_sem.at[1])
     messages = recv_m[...].astype(F32).reshape(64, 128).astype(BF16)
@@ -229,7 +262,7 @@
     part_buf[...] = columns.astype(BF16).reshape(4, 32, 128)
 
     for i in range(1, 4):
-        to = lax.rem(h + i, 4)
+        to = h ^ i
         pltpu.make_async_remote_copy(
             part_buf.at[to], recv_r.at[h], send_sem.at[3], recv_sem.at[3], (d, to), MESH
         ).start()
@@ -245,84 +278,136 @@
         .reshape(8, 16, 128)
     )
 
-    def send_slots(i, carry):
-        to = lax.rem(me + i, 128)
-        pltpu.make_async_remote_copy(
-            sel_buf.at[to // 16],
-            recv_b.at[me],
-            send_sem.at[4],
-            recv_sem.at[4],
-            device(to),
-            MESH,
-        ).start()
-        return carry
-
-    lax.fori_loop(1, 128, send_slots, 0)
-    pltpu.make_async_copy(sel_buf.at[me // 16], recv_b.at[me], recv_sem.at[4]).start()
-
-    def send_stream(b, carry):
-        to = h * 8 + b
-        here = (to == d) & (quarter == h)
-
-        @pl.when(here)
+    slot = block
+    for i in FAR + [0]:
+        to = d ^ i
+        for side in range(2):
+            place = recv_b.at[c, (i & 24) + slot, y]
+
+            def remote():
+                pltpu.make_async_remote_copy(
+                    sel_buf.at[to >> 2],
+                    place,
+                    send_sem.at[4],
+                    group_sem.at[i >> 3],
+                    (to, side * 2 + c),
+                    MESH,
+                ).start()
+
+            if i:
+                remote()
+            else:
+                pl.when(y != side)(remote)
+    pltpu.make_async_copy(sel_buf.at[d >> 2], recv_b.at[c, slot, y], group_sem.at[0]).start()
+
+    for b in range(8):
+        own_place = here & (h * 8 + b == d)
+
+        @pl.when(own_place)
         def _():
             pltpu.make_async_copy(
                 stream_buf.at[b // 2], recv_s.at[block], recv_sem.at[5]
             ).start()
 
-        @pl.when(jnp.logical_not(here))
+        @pl.when(jnp.logical_not(own_place))
         def _():
             pltpu.make_async_remote_copy(
                 stream_buf.at[b // 2],
                 recv_s.at[block],
                 send_sem.at[5],
                 recv_sem.at[5],
-                (to, quarter),
+                (h * 8 + b, quarter),
                 MESH,
             ).start()
-
-        return carry
-
-    lax.fori_loop(0, 8, send_stream, 0)
 
     pltpu.make_async_copy(win_hbm.at[0], win_buf, w_sem.at[1]).wait()
     pltpu.make_async_copy(wdown_hbm.at[0], wdown_buf, w_sem.at[2]).wait()
     whole_wait(recv_g, recv_sem.at[2])
-    whole_wait(recv_b, recv_sem.at[4])
+
+    def hand_on(k):
+        return pltpu.make_async_remote_copy(
+            recv_b.at[c, pl.ds(k * 8, 8)],
+            recv_b.at[c, pl.ds(k * 8, 8)],
+            pass_send.at[k],
+            pass_recv.at[k],
+            sibling,
+            MESH,
+        )
+
+    def arrived(k):
+        whole_wait(recv_b.at[c, pl.ds(k * 8, 8)], group_sem.at[k])
+        hand_on(k).start()
+
     squares = jnp.zeros((64, 128), F32)
-    for n in range(32):
-        x = recv_b[n * 4 : (n + 1) * 4].reshape(64, 128).astype(F32)
-        squares = squares + x * x
-        x_buf[:, n * 128 : (n + 1) * 128] = (
-            x * recv_g[n // 8, n % 8 : n % 8 + 1, :]
-        ).astype(BF16)
+    gate = jnp.zeros((64, 448), F32)
+    up = jnp.zeros((64, 448), F32)
+    arrived(ORDER[0])
+    for n in range(4):
+        k = ORDER[n]
+        if n < 3:
+            arrived(ORDER[n + 1])
+        whole_wait(recv_b.at[1 - c, pl.ds(k * 8, 8)], pass_recv.at[k])
+        first = quarter ^ k
+        gains = recv_g[pl.ds(pl.multiple_of(first * 8, 8), 8), :]
+        for m in range(8):
+            x = recv_b[:, k * 8 + m].reshape(64, 128).astype(F32)
+            squares = squares + x * x
+            x_buf[:, m * 128 : (m + 1) * 128] = (x * gains[m : m + 1]).astype(BF16)
+        columns = pl.ds(pl.multiple_of(first * 1024, 1024), 1024)
+        x = x_buf[...]
+        gate = gate + lax.dot_general(x, win_buf[0, :, columns], nt, preferred_element_type=F32)
+        up = up + lax.dot_general(x, win_buf[1, :, columns], nt, preferred_element_type=F32)
     inverse = lax.rsqrt(jnp.sum(squares, axis=1, keepdims=True) * (1.0 / 4096.0) + EPSILON)
-    gate = lax.dot_general(x_buf[...], win_buf[0], nt, preferred_element_type=F32) * inverse
-    up = lax.dot_general(x_buf[...], win_buf[1], nt, preferred_element_type=F32) * inverse
-    hidden = (gate * jax.nn.sigmoid(gate) * up).astype(BF16)
-    for n in range(16):
-        slab = jnp.dot(
-            hidden, wdown_buf[:, n * 256 : (n + 1) * 256], preferred_element_type=F32
+    gate = gate * inverse
+    hidden = (gate * jax.nn.sigmoid(gate) * (up * inverse)).astype(BF16)
+
+    def slab(side, core):
+        base = (side * 2 + core) * 1024
+        for n in range(4):
+            columns = pl.ds(pl.multiple_of(base + n * 256, 256), 256)
+            part = jnp.dot(hidden, wdown_buf[:, columns], preferred_element_type=F32)
+            for m in range(2):
+                slab_f[pl.ds(n * 2 + m, 64, stride=8), :] = part[:, m * 128 : (m + 1) * 128]
+        return slab_f[...]
+
+    def to_sibling(side):
+        return pltpu.make_async_remote_copy(
+            sib_buf.at[side],
+            recv_d.at[side],
+            sib_send.at[side],
+            sib_recv.at[side],
+            sibling,
+            MESH,
         )
-        for m in range(2):
-            j = (n * 2 + m) % 8
-            slab_f[n // 4, pl.ds(j, 64, stride=8), :] = slab[:, m * 128 : (m + 1) * 128]
-    slab_b[...] = slab_f[...].astype(BF16).reshape(4, 32, 16, 128)
-
-    def send_back(i, carry):
-        to = lax.rem(me + i, 128)
-        pltpu.make_async_remote_copy(
-            slab_b.at[lax.rem(to, 4), to // 4],
-            recv_c.at[me],
-            send_sem.at[6],
-            recv_sem.at[6],
-            device(to),
-            MESH,
-        ).start()
-        return carry
-
-    lax.fori_loop(1, 128, send_back, 0)
-    pltpu.make_async_copy(slab_b.at[h, d], recv_c.at[me], recv_sem.at[6]).start()
+
+    for side in range(2):
+        sib_buf[side] = slab(side, 1 - c).astype(BF16)
+        to_sibling(side).start()
+    for side in range(2):
+        total = slab(side, c)
+        to_sibling(side).wait_recv()
+        total = total + recv_d[side].astype(F32)
+        slab_b[side] = total.astype(BF16).reshape(32, 16, 128)
+        for i in FAR + [0]:
+            to = d ^ i
+            rows = ((to >> 3) & 1) * 16 + (to >> 4) * 8 + (to & 7)
+
+            def remote():
+                pltpu.make_async_remote_copy(
+                    slab_b.at[side, rows],
+                    recv_c.at[d * 2 + y],
+                    send_sem.at[6],
+                    recv_sem.at[6],
+                    (to, side * 2 + c),
+                    MESH,
+                ).start()
+
+            if i:
+                remote()
+            else:
+                pl.when(y != side)(remote)
+    rows = ((d >> 3) & 1) * 16 + (d >> 4) * 8 + (d & 7)
+    pltpu.make_async_copy(slab_b.at[y, rows], recv_c.at[d * 2 + y], recv_sem.at[6]).start()
 
     slot16 = lax.broadcasted_iota(I32, (16, 128), 0)
     factors = []
@@ -332,14 +417,14 @@
             a = t * 2 + j
             factor = factor + jnp.where(slot16 == ids[a] * 2 + slots[a], gates_ref[j, t], 0.0)
         factors.append(factor)
-    odd = lax.rem(d, 2) == 1
+    odd = (d & 1) == 1
 
     whole_wait(recv_s, recv_sem.at[5])
     whole_wait(recv_c, recv_sem.at[6])
     for e in range(8):
-        total = recv_c[e * 16].astype(F32)
-        for i in range(1, 16):
-            total = total + recv_c[e * 16 + i].astype(F32)
+        total = recv_c[e * 8].astype(F32)
+        for i in range(1, 8):
+            total = total + recv_c[e * 8 + i].astype(F32)
         mix_f[e * 16 : (e + 1) * 16, :] = total
     for j in range(8):
         slot_rows = mix_f[pl.ds(j, 16, stride=8), :]
@@ -350,23 +435,29 @@
         own_stream = jnp.where(odd, own_stream[4:], own_stream[:4])
         out_ref[:, j * 128 : (j + 1) * 128] = (own_stream + mixed).astype(BF16)
 
+    result = pltpu.make_async_copy(out_ref, out_hbm, w_sem.at[0])
+    result.start()
     whole_wait(recv_a.at[pl.ds(0, 31)], send_sem.at[0])
-    apart = (quarter != h).astype(I32)
-
-    @pl.when(quarter == h)
+
+    @pl.when(here)
     def _():
         whole_wait(recv_m.at[pl.ds(0, 7)], send_sem.at[1])
         whole_wait(recv_s.at[pl.ds(0, 7)], send_sem.at[5])
 
-    @pl.when(quarter != h)
+    @pl.when(jnp.logical_not(here))
     def _():
         whole_wait(recv_m, send_sem.at[1])
         whole_wait(recv_s, send_sem.at[5])
 
-    whole_wait(recv_g.at[pl.ds(0, 3)], send_sem.at[2])
+    whole_wait(recv_g.at[pl.ds(0, 24)], send_sem.at[2])
     whole_wait(recv_r.at[pl.ds(0, 3)], send_sem.at[3])
-    whole_wait(recv_b.at[pl.ds(0, 127)], send_sem.at[4])
-    whole_wait(recv_c.at[pl.ds(0, 127)], send_sem.at[6])
+    whole_wait(recv_c.at[pl.ds(0, 63)], send_sem.at[4])
+    whole_wait(recv_c.at[pl.ds(0, 63)], send_sem.at[6])
+    for k in range(4):
+        hand_on(k).wait_send()
+    for side in range(2):
+        to_sibling(side).wait_send()
+    result.wait()
 
 
 def shards(
@@ -385,15 +476,24 @@
     w_in,
     w_down,
 ):
-    smem = pl.BlockSpec(memory_space=pltpu.SMEM)
-    vmem = pl.BlockSpec(memory_space=pltpu.VMEM)
     hbm = pl.BlockSpec(memory_space=pltpu.HBM)
+    gain = norm_gain.reshape(8, 128)
     return pl.pallas_call(
         layer,
         out_shape=jax.ShapeDtypeStruct((4, 1024), BF16),
-        in_specs=[smem] * 3 + [vmem] * 6 + [hbm] * 5,
-        out_specs=vmem,
+        in_specs=[hbm] * 14,
+        out_specs=pl.BlockSpec(memory_space=OUT_SPACE),
         scratch_shapes=[
+            pltpu.SMEM((2, 4), I32),
+            pltpu.SMEM((2, 4), F32),
+            pltpu.SMEM((4,), I32),
+            pltpu.VMEM(residual.shape, BF16),
+            pltpu.VMEM(query.shape, BF16),
+            pltpu.VMEM(fresh_token_keys.shape, BF16),
+            pltpu.VMEM(value_new.shape, BF16),
+            pltpu.VMEM(pages.shape, I32),
+            pltpu.VMEM(gain.shape, F32),
+            pltpu.VMEM((4, 1024), BF16),
             pltpu.VMEM((4, 2, 2048, 128), BF16),
             pltpu.VMEM((4, 2, 2048, 128), BF16),
             pltpu.VMEM((1024, 128), BF16),
@@ -404,25 +504,33 @@
             pltpu.VMEM((1024, 128), F32),
             pltpu.VMEM((8, 8, 128), BF16),
             pltpu.VMEM((8, 8, 128), BF16),
-            pltpu.VMEM((4, 8, 128), F32),
+            pltpu.VMEM((32, 128), F32),
             pltpu.VMEM((4, 32, 128), BF16),
             pltpu.VMEM((4, 32, 128), BF16),
             pltpu.VMEM((4, 8, 128), F32),
             pltpu.VMEM((8, 16, 128), BF16),
-            pltpu.VMEM((128, 16, 128), BF16),
+            pltpu.VMEM((2, 32, 2, 16, 128), BF16),
             pltpu.VMEM((8, 8, 128), F32),
-            pltpu.VMEM((64, 4096), BF16),
-            pltpu.VMEM((4, 512, 128), F32),
-            pltpu.VMEM((4, 32, 16, 128), BF16),
-            pltpu.VMEM((128, 16, 128), BF16),
+            pltpu.VMEM((64, 1024), BF16),
+            pltpu.VMEM((512, 128), F32),
+            pltpu.VMEM((2, 512, 128), BF16),
+            pltpu.VMEM((2, 512, 128), BF16),
+            pltpu.VMEM((2, 32, 16, 128), BF16),
+            pltpu.VMEM((64, 16, 128), BF16),
             pltpu.VMEM((128, 128), F32),
+            pltpu.SemaphoreType.DMA((9,)),
             pltpu.SemaphoreType.DMA((2, 4)),
             pltpu.SemaphoreType.DMA((3,)),
             pltpu.SemaphoreType.DMA((7,)),
             pltpu.SemaphoreType.DMA((7,)),
+            pltpu.SemaphoreType.DMA((4,)),
+            pltpu.SemaphoreType.DMA((4,)),
+            pltpu.SemaphoreType.DMA((4,)),
+            pltpu.SemaphoreType.DMA((2,)),
+            pltpu.SemaphoreType.DMA((2,)),
         ],
         compiler_params=pltpu.CompilerParams(
-            collective_id=0, has_side_effects=True, vmem_limit_bytes=60 * 1024 * 1024
+            collective_id=0, has_side_effects=True, vmem_limit_bytes=67043328
         ),
         name="layer",
     )(
@@ -434,7 +542,7 @@
         fresh_token_keys,
         value_new,
         pages,
-        norm_gain.reshape(8, 128),
+        gain,
         key_cache,
         value_cache,
         w_out,

time: 49.4 us -> 41.3 us (0.84)
  Pallas kernels: 47.9 us -> 39.6 us
    pallas_call x1, Pallas kernels: 47.9 us -> 39.6 us  [shards(): pl.pallas_call(layer, out_shape=jax.ShapeDtypeStruct((4, 1024), BF16), in...]
where the time goes in v3:
time: 41.3 us; the launch traced here: 40.9 us
  Pallas kernels  39.6 us (96%)
  local copies, waits for them, and re-layouts  1.3 us (3%)
    pallas_call x1, Pallas kernels, shards(): pl.pallas_call(layer, out_shape=jax.ShapeDtypeStruct((4, 1024), BF16), in...  39.6 us
    unnamed x1, local copies, waits for them, and re-layouts  1.3 us

profile of v3, /device:TPU:1, one launch (start us, length us, event | category | flops | bytes accessed | tf_op | source)
XLA Modules:
  0.0 40.9 jit_solution(11111953688615014252)
XLA Ops:
  0.0 39.6 %layer.1 = bf16[4,1024]{1,0:T(4,128)(2,1)} custom-call(s32[2,4]{1,0:T(2,128)} %bitcast.6, f32[2,4]{1,0:T(2,128)} %bitcast.7, s32[4]{0:T(128)} %len_hbm.1, bf16[4,1024]{1,0:T(4,128)(2,1)} %residual_hbm.1, bf16[4,8,128]{2,1,0:T(8,128)(2,1)} %query_hbm.1, bf16[4,2,128]{2,1,0:T(2,128)(2,1)} %fresh_hbm.1, bf16[4,2,128]{2,1,0:T(2,128)(2,1)} %vnew_hbm.1, ...), custom_call_target="tpu_custom_call" | custom-call | tf_op jit(solution)/shard_map/layer/pallas_call | solution.py:481
  39.6 1.3 %copy.16 = bf16[4,1024]{1,0:T(4,128)(2,1)} copy(bf16[4,1024]{1,0:T(4,128)(2,1)} %layer.1) | data formatting | bytes 16384

commit v4 on v3

--- a/solution.py
+++ b/solution.py
@@ -42,6 +42,7 @@
     ids_ref,
     gates_ref,
     len_ref,
+    page_list,
     residual_ref,
     query_ref,
     fresh_ref,
@@ -49,8 +50,14 @@
     pages_ref,
     gain_ref,
     out_ref,
-    key_buf,
-    value_buf,
+    key0,
+    key1,
+    key2,
+    key3,
+    value0,
+    value1,
+    value2,
+    value3,
     wout_buf,
     win_buf,
     wdown_buf,
@@ -60,6 +67,7 @@
     msg_buf,
     recv_m,
     recv_g,
+    part_f,
     part_buf,
     recv_r,
     stream_buf,
@@ -68,6 +76,7 @@
     recv_s,
     x_buf,
     slab_f,
+    own_f,
     sib_buf,
     recv_d,
     slab_b,
@@ -78,6 +87,7 @@
     w_sem,
     send_sem,
     recv_sem,
+    half_sem,
     group_sem,
     pass_send,
     pass_recv,
@@ -101,6 +111,7 @@
         (ids_hbm, ids_ref),
         (gates_hbm, gates_ref),
         (len_hbm, len_ref),
+        (pages_hbm, page_list),
         (pages_hbm, pages_ref),
         (query_hbm, query_ref),
         (fresh_hbm, fresh_ref),
@@ -111,6 +122,17 @@
     for n, (source, target) in enumerate(small):
         pltpu.make_async_copy(source, target, in_sem.at[n]).start()
 
+    keys = [key0, key1, key2, key3]
+    values = [value0, value1, value2, value3]
+
+    def load_keys(b):
+        return pltpu.make_async_copy(key_hbm.at[b], keys[b], kv_sem.at[0, b])
+
+    def load_values(b):
+        return pltpu.make_async_copy(value_hbm.at[b], values[b], kv_sem.at[1, b])
+
+    load_keys(0).start()
+
     for i in FAR:
         for side in range(2):
             greet((d ^ i, side * 2 + c))
@@ -122,9 +144,13 @@
         def _():
             greet((h * 8 + j, quarter))
 
-    for b in range(4):
-        pltpu.make_async_copy(key_hbm.at[b], key_buf.at[b], kv_sem.at[0, b]).start()
-        pltpu.make_async_copy(value_hbm.at[b], value_buf.at[b], kv_sem.at[1, b]).start()
+    load_keys(1).start()
+    load_values(0).start()
+    load_values(1).start()
+    load_keys(2).start()
+    load_keys(3).start()
+    load_values(2).start()
+    load_values(3).start()
     for n, (source, target) in enumerate(small):
         pltpu.make_async_copy(source, target, in_sem.at[n]).wait()
 
@@ -149,57 +175,77 @@
         both = jnp.concatenate([res, jnp.zeros((4, 128), F32)], axis=0)
         msg_buf[j] = (both + target).astype(BF16)
 
-    head_lane = lax.broadcasted_iota(I32, (128, 128), 1)
-    page_row = lax.broadcasted_iota(I32, (128, 64), 0)
-    chosen = jnp.zeros((128, 128), F32)
-    for b in range(4):
-        for k in range(2):
-            hit = (pages_ref[b, k : k + 1, :] == page_row).astype(F32)
-            column = jnp.sum(hit, axis=1, keepdims=True)
-            chosen = jnp.where((head_lane >> 2) == b * 2 + k, column, chosen)
-    chosen_rows = chosen.T[:32, :].astype(BF16)
+    top_rows = lax.broadcasted_iota(I32, (8, 1), 0) < 4
+    numbers = jnp.concatenate(
+        [jnp.where(top_rows, pages_ref[b, 0:1, :], pages_ref[b, 1:2, :]) for b in range(4)],
+        axis=0,
+    )
     spread = (
-        (lax.broadcasted_iota(I32, (128, 2048), 1) >> 4)
-        == lax.broadcasted_iota(I32, (128, 2048), 0)
-    ).astype(F32).astype(BF16)
-    mask = jnp.dot(chosen_rows, spread, preferred_element_type=F32)
-
-    position = lax.broadcasted_iota(I32, (8, 2048), 1)
-    top_rows = lax.broadcasted_iota(I32, (8, 1), 0) < 4
+        (lax.broadcasted_iota(I32, (64, 1024), 1) >> 4)
+        == lax.broadcasted_iota(I32, (64, 1024), 0)
+    ).astype(F32)
+    start = jnp.dot(
+        numbers.astype(F32).astype(BF16), spread.astype(BF16), preferred_element_type=F32
+    )
+    position = start.astype(I32) * PAGE + (lax.broadcasted_iota(I32, (32, 1024), 1) & 15)
+
     scale = 128.0 ** (-0.5)
     nt = (((1,), (1,)), ((), ()))
-    for b in range(4):
-        q = query_ref[b]
-        qf = q.astype(F32)
-        fresh = jnp.where(
-            top_rows, fresh_ref[b, 0:1, :].astype(F32), fresh_ref[b, 1:2, :].astype(F32)
+
+    def selected(buf, b, k):
+        return jnp.concatenate([buf[k, page_list[b, k, n]] for n in range(64)], axis=0)
+
+    def both(ref, b):
+        return jnp.where(top_rows, ref[b, 0:1, :].astype(F32), ref[b, 1:2, :].astype(F32))
+
+    def attend(pair):
+        rows = jnp.concatenate([query_ref[b] for b in pair], axis=0).astype(F32)
+        fresh = jnp.concatenate([both(fresh_ref, b) for b in pair], axis=0)
+        own = jnp.sum(rows * fresh, axis=1, keepdims=True) * scale
+        live = jnp.concatenate(
+            [position[b * 8 : (b + 1) * 8] < len_ref[b] for b in pair], axis=0
         )
-        own = jnp.sum(qf * fresh, axis=1, keepdims=True) * scale
-        live = (mask[b * 8 : (b + 1) * 8] > 0.5) & (position < len_ref[b])
-        pltpu.make_async_copy(key_hbm.at[b], key_buf.at[b], kv_sem.at[0, b]).wait()
-        s0 = lax.dot_general(q, key_buf[b, 0], nt, preferred_element_type=F32)
-        s1 = lax.dot_general(q, key_buf[b, 1], nt, preferred_element_type=F32)
-        scores = jnp.where(top_rows, s0, s1) * scale
+        for b in pair:
+            load_keys(b).wait()
+        scores = []
+        for b in pair:
+            q = query_ref[b]
+            s0 = lax.dot_general(q, selected(keys[b], b, 0), nt, preferred_element_type=F32)
+            s1 = lax.dot_general(q, selected(keys[b], b, 1), nt, preferred_element_type=F32)
+            scores.append(jnp.where(top_rows, s0, s1))
+        scores = jnp.concatenate(scores, axis=0) * scale
         masked = jnp.where(live, scores, -1e30)
         top = jnp.maximum(jnp.max(masked, axis=1, keepdims=True), own)
         expo = jnp.where(live, jnp.exp(scores - top), 0.0)
         own_expo = jnp.exp(own - top)
         total = jnp.sum(expo, axis=1, keepdims=True) + own_expo
-        weights = (expo / total).astype(BF16)
+        weights = expo / total
         own_weight = (own_expo / total).astype(BF16).astype(F32)
-        pltpu.make_async_copy(value_hbm.at[b], value_buf.at[b], kv_sem.at[1, b]).wait()
-        a0 = jnp.dot(weights, value_buf[b, 0], preferred_element_type=F32)
-        a1 = jnp.dot(weights, value_buf[b, 1], preferred_element_type=F32)
-        new = jnp.where(
-            top_rows, vnew_ref[b, 0:1, :].astype(F32), vnew_ref[b, 1:2, :].astype(F32)
-        )
-        attn_buf[b * 8 : (b + 1) * 8, :] = (
-            jnp.where(top_rows, a0, a1) + own_weight * new
-        ).astype(BF16)
-
-    pltpu.make_async_copy(wout_hbm, wout_buf, w_sem.at[0]).start()
-    pltpu.make_async_copy(win_hbm.at[0], win_buf, w_sem.at[1]).start()
-    pltpu.make_async_copy(wdown_hbm.at[0], wdown_buf, w_sem.at[2]).start()
+        for b in pair:
+            load_values(b).wait()
+        for n, b in enumerate(pair):
+            w = weights[n * 8 : (n + 1) * 8].astype(BF16)
+            a0 = jnp.dot(w, selected(values[b], b, 0), preferred_element_type=F32)
+            a1 = jnp.dot(w, selected(values[b], b, 1), preferred_element_type=F32)
+            new = own_weight[n * 8 : (n + 1) * 8] * both(vnew_ref, b)
+            attn_buf[b // 2, n * 8 : (n + 1) * 8, :] = (
+                jnp.where(top_rows, a0, a1) + new
+            ).astype(BF16)
+
+    def send_rows(half):
+        for i in FAR:
+            pltpu.make_async_remote_copy(
+                attn_buf.at[half],
+                recv_a.at[half, d],
+                send_sem.at[0],
+                half_sem.at[half],
+                (d ^ i, h),
+                MESH,
+            ).start()
+        pltpu.make_async_copy(attn_buf.at[half], recv_a.at[half, d], half_sem.at[half]).start()
+
+    attend((0, 1))
+    attend((2, 3))
     here = quarter == h
     pl.semaphore_wait(barrier, 73 - here.astype(I32))
     for j in range(8):
@@ -220,11 +266,11 @@
                 MESH,
             ).start()
 
-    for i in FAR:
-        pltpu.make_async_remote_copy(
-            attn_buf, recv_a.at[d], send_sem.at[0], recv_sem.at[0], (d ^ i, h), MESH
-        ).start()
-    pltpu.make_async_copy(attn_buf, recv_a.at[d], recv_sem.at[0]).start()
+    send_rows(0)
+    send_rows(1)
+    pltpu.make_async_copy(wout_hbm, wout_buf, w_sem.at[0]).start()
+    pltpu.make_async_copy(win_hbm.at[0], win_buf, w_sem.at[1]).start()
+    pltpu.make_async_copy(wdown_hbm.at[0], wdown_buf, w_sem.at[2]).start()
 
     own_gains = recv_g.at[pl.ds(pl.multiple_of(h * 8, 8), 8)]
     for i in range(1, 4):
@@ -249,17 +295,28 @@
     select = select[:, :32].astype(BF16)
     pltpu.make_async_copy(wout_hbm, wout_buf, w_sem.at[0]).wait()
 
-    whole_wait(recv_a, recv_sem.at[0])
-    rows_f[...] = recv_a[...].astype(F32).reshape(1024, 128)
-    columns = jnp.zeros((128, 128), F32)
-    for n in range(4):
-        pair = jnp.concatenate(
-            [rows_f[pl.ds(n * 2 + m, 128, stride=8), :] for m in range(2)], axis=1
-        ).astype(BF16)
-        columns = columns + jnp.dot(
-            pair, wout_buf[n * 256 : (n + 1) * 256, :], preferred_element_type=F32
-        )
-    part_buf[...] = columns.astype(BF16).reshape(4, 32, 128)
+    def project(half):
+        whole_wait(recv_a.at[half], half_sem.at[half])
+        rows_f[...] = recv_a[half].astype(F32).reshape(512, 128)
+        columns = jnp.zeros((64, 128), F32)
+        for n in range(4):
+            pair = [
+                jnp.concatenate(
+                    [rows_f[pl.ds(t * 8 + n * 2 + m, 32, stride=16), :] for t in range(2)], axis=0
+                )
+                for m in range(2)
+            ]
+            columns = columns + jnp.dot(
+                jnp.concatenate(pair, axis=1).astype(BF16),
+                wout_buf[n * 256 : (n + 1) * 256, :],
+                preferred_element_type=F32,
+            )
+        for t in range(2):
+            part_f[pl.ds(half * 2 + t, 32, stride=4), :] = columns[t * 32 : (t + 1) * 32]
+
+    project(0)
+    project(1)
+    part_buf[...] = part_f[...].astype(BF16).reshape(4, 32, 128)
 
     for i in range(1, 4):
         to = h ^ i
@@ -279,7 +336,7 @@
     )
 
     slot = block
-    for i in FAR + [0]:
+    for i in range(32):
         to = d ^ i
         for side in range(2):
             place = recv_b.at[c, (i & 24) + slot, y]
@@ -384,9 +441,10 @@
         sib_buf[side] = slab(side, 1 - c).astype(BF16)
         to_sibling(side).start()
     for side in range(2):
-        total = slab(side, c)
+        own_f[side] = slab(side, c)
+    for side in range(2):
         to_sibling(side).wait_recv()
-        total = total + recv_d[side].astype(F32)
+        total = own_f[side] + recv_d[side].astype(F32)
         slab_b[side] = total.astype(BF16).reshape(32, 16, 128)
         for i in FAR + [0]:
             to = d ^ i
@@ -437,7 +495,8 @@
 
     result = pltpu.make_async_copy(out_ref, out_hbm, w_sem.at[0])
     result.start()
-    whole_wait(recv_a.at[pl.ds(0, 31)], send_sem.at[0])
+    for half in range(2):
+        whole_wait(recv_a.at[half, pl.ds(0, 31)], send_sem.at[0])
 
     @pl.when(here)
     def _():
@@ -487,6 +546,7 @@
             pltpu.SMEM((2, 4), I32),
             pltpu.SMEM((2, 4), F32),
             pltpu.SMEM((4,), I32),
+            pltpu.SMEM(pages.shape, I32),
             pltpu.VMEM(residual.shape, BF16),
             pltpu.VMEM(query.shape, BF16),
             pltpu.VMEM(fresh_token_keys.shape, BF16),
@@ -494,17 +554,19 @@
             pltpu.VMEM(pages.shape, I32),
             pltpu.VMEM(gain.shape, F32),
             pltpu.VMEM((4, 1024), BF16),
-            pltpu.VMEM((4, 2, 2048, 128), BF16),
-            pltpu.VMEM((4, 2, 2048, 128), BF16),
+        ]
+        + [pltpu.VMEM((2, 128, PAGE, 128), BF16)] * 8
+        + [
             pltpu.VMEM((1024, 128), BF16),
             pltpu.VMEM((2, 448, 4096), BF16),
             pltpu.VMEM((448, 4096), BF16),
-            pltpu.VMEM((32, 128), BF16),
-            pltpu.VMEM((32, 32, 128), BF16),
-            pltpu.VMEM((1024, 128), F32),
+            pltpu.VMEM((2, 16, 128), BF16),
+            pltpu.VMEM((2, 32, 16, 128), BF16),
+            pltpu.VMEM((512, 128), F32),
             pltpu.VMEM((8, 8, 128), BF16),
             pltpu.VMEM((8, 8, 128), BF16),
             pltpu.VMEM((32, 128), F32),
+            pltpu.VMEM((128, 128), F32),
             pltpu.VMEM((4, 32, 128), BF16),
             pltpu.VMEM((4, 32, 128), BF16),
             pltpu.VMEM((4, 8, 128), F32),
@@ -513,16 +575,18 @@
             pltpu.VMEM((8, 8, 128), F32),
             pltpu.VMEM((64, 1024), BF16),
             pltpu.VMEM((512, 128), F32),
+            pltpu.VMEM((2, 512, 128), F32),
             pltpu.VMEM((2, 512, 128), BF16),
             pltpu.VMEM((2, 512, 128), BF16),
             pltpu.VMEM((2, 32, 16, 128), BF16),
             pltpu.VMEM((64, 16, 128), BF16),
             pltpu.VMEM((128, 128), F32),
-            pltpu.SemaphoreType.DMA((9,)),
+            pltpu.SemaphoreType.DMA((10,)),
             pltpu.SemaphoreType.DMA((2, 4)),
             pltpu.SemaphoreType.DMA((3,)),
             pltpu.SemaphoreType.DMA((7,)),
             pltpu.SemaphoreType.DMA((7,)),
+            pltpu.SemaphoreType.DMA((2,)),
             pltpu.SemaphoreType.DMA((4,)),
             pltpu.SemaphoreType.DMA((4,)),
             pltpu.SemaphoreType.DMA((4,)),
@@ -543,8 +607,8 @@
         value_new,
         pages,
         gain,
-        key_cache,
-        value_cache,
+        key_cache.reshape(4, 2, 128, PAGE, 128),
+        value_cache.reshape(4, 2, 128, PAGE, 128),
         w_out,
         jnp.swapaxes(w_in, 2, 3),
         w_down,

time: 41.3 us -> 40.5 us (0.981)
  Pallas kernels: 39.6 us -> 39 us
    pallas_call x1, Pallas kernels: 39.6 us -> 39 us  [shards(): pl.pallas_call(layer, out_shape=jax.ShapeDtypeStruct((4, 1024), BF16), in...]
where the time goes in v4:
time: 40.5 us; the launch traced here: 40.4 us
  Pallas kernels  39 us (96%)
  local copies, waits for them, and re-layouts  1.3 us (3%)
    pallas_call x1, Pallas kernels, shards(): pl.pallas_call(layer, out_shape=jax.ShapeDtypeStruct((4, 1024), BF16), in...  39 us
    unnamed x1, local copies, waits for them, and re-layouts  1.3 us

profile of v4, /device:TPU:1, one launch (start us, length us, event | category | flops | bytes accessed | tf_op | source)
XLA Modules:
  0.0 40.4 jit_solution(5932305926630892255)
XLA Ops:
  0.0 39.0 %layer.1 = bf16[4,1024]{1,0:T(4,128)(2,1)} custom-call(s32[2,4]{1,0:T(2,128)} %bitcast.10, f32[2,4]{1,0:T(2,128)} %bitcast.11, s32[4]{0:T(128)} %len_hbm.1, bf16[4,1024]{1,0:T(4,128)(2,1)} %residual_hbm.1, bf16[4,8,128]{2,1,0:T(8,128)(2,1)} %query_hbm.1, bf16[4,2,128]{2,1,0:T(2,128)(2,1)} %fresh_hbm.1, bf16[4,2,128]{2,1,0:T(2,128)(2,1)} %vnew_hbm.1, ...), custom_call_target="tpu_custom_call" | custom-call | tf_op jit(solution)/shard_map/layer/pallas_call | solution.py:540
  39.1 1.3 %copy.16 = bf16[4,1024]{1,0:T(4,128)(2,1)} copy(bf16[4,1024]{1,0:T(4,128)(2,1)} %layer.1) | data formatting | bytes 16384

commit v5 on v4

--- a/solution.py
+++ b/solution.py
@@ -60,6 +60,7 @@
     value3,
     wout_buf,
     win_buf,
+    turned,
     wdown_buf,
     attn_buf,
     recv_a,
@@ -67,7 +68,6 @@
     msg_buf,
     recv_m,
     recv_g,
-    part_f,
     part_buf,
     recv_r,
     stream_buf,
@@ -87,7 +87,6 @@
     w_sem,
     send_sem,
     recv_sem,
-    half_sem,
     group_sem,
     pass_send,
     pass_recv,
@@ -132,6 +131,7 @@
         return pltpu.make_async_copy(value_hbm.at[b], values[b], kv_sem.at[1, b])
 
     load_keys(0).start()
+    load_keys(1).start()
 
     for i in FAR:
         for side in range(2):
@@ -144,13 +144,10 @@
         def _():
             greet((h * 8 + j, quarter))
 
-    load_keys(1).start()
-    load_values(0).start()
-    load_values(1).start()
-    load_keys(2).start()
-    load_keys(3).start()
-    load_values(2).start()
-    load_values(3).start()
+    for b in range(2, 4):
+        load_keys(b).start()
+    for b in range(4):
+        load_values(b).start()
     for n, (source, target) in enumerate(small):
         pltpu.make_async_copy(source, target, in_sem.at[n]).wait()
 
@@ -205,10 +202,9 @@
         live = jnp.concatenate(
             [position[b * 8 : (b + 1) * 8] < len_ref[b] for b in pair], axis=0
         )
+        scores = []
         for b in pair:
             load_keys(b).wait()
-        scores = []
-        for b in pair:
             q = query_ref[b]
             s0 = lax.dot_general(q, selected(keys[b], b, 0), nt, preferred_element_type=F32)
             s1 = lax.dot_general(q, selected(keys[b], b, 1), nt, preferred_element_type=F32)
@@ -221,31 +217,27 @@
         total = jnp.sum(expo, axis=1, keepdims=True) + own_expo
         weights = expo / total
         own_weight = (own_expo / total).astype(BF16).astype(F32)
-        for b in pair:
+        for n, b in enumerate(pair):
             load_values(b).wait()
-        for n, b in enumerate(pair):
             w = weights[n * 8 : (n + 1) * 8].astype(BF16)
             a0 = jnp.dot(w, selected(values[b], b, 0), preferred_element_type=F32)
             a1 = jnp.dot(w, selected(values[b], b, 1), preferred_element_type=F32)
             new = own_weight[n * 8 : (n + 1) * 8] * both(vnew_ref, b)
-            attn_buf[b // 2, n * 8 : (n + 1) * 8, :] = (
+            attn_buf[n * 8 : (n + 1) * 8, :] = (
                 jnp.where(top_rows, a0, a1) + new
             ).astype(BF16)
 
-    def send_rows(half):
+    def send_rows():
         for i in FAR:
             pltpu.make_async_remote_copy(
-                attn_buf.at[half],
-                recv_a.at[half, d],
-                send_sem.at[0],
-                half_sem.at[half],
-                (d ^ i, h),
-                MESH,
+                attn_buf, recv_a.at[d], send_sem.at[0], recv_sem.at[0], (d ^ i, h), MESH
             ).start()
-        pltpu.make_async_copy(attn_buf.at[half], recv_a.at[half, d], half_sem.at[half]).start()
-
-    attend((0, 1))
-    attend((2, 3))
+        pltpu.make_async_copy(attn_buf, recv_a.at[d], recv_sem.at[0]).start()
+
+    attend(range(4))
+    pltpu.make_async_copy(wout_hbm, wout_buf, w_sem.at[0]).start()
+    pltpu.make_async_copy(win_hbm.at[0], win_buf, w_sem.at[1]).start()
+    pltpu.make_async_copy(wdown_hbm.at[0], wdown_buf, w_sem.at[2]).start()
     here = quarter == h
     pl.semaphore_wait(barrier, 73 - here.astype(I32))
     for j in range(8):
@@ -266,11 +258,7 @@
                 MESH,
             ).start()
 
-    send_rows(0)
-    send_rows(1)
-    pltpu.make_async_copy(wout_hbm, wout_buf, w_sem.at[0]).start()
-    pltpu.make_async_copy(win_hbm.at[0], win_buf, w_sem.at[1]).start()
-    pltpu.make_async_copy(wdown_hbm.at[0], wdown_buf, w_sem.at[2]).start()
+    send_rows()
 
     own_gains = recv_g.at[pl.ds(pl.multiple_of(h * 8, 8), 8)]
     for i in range(1, 4):
@@ -278,6 +266,17 @@
             gain_ref, own_gains, send_sem.at[2], recv_sem.at[2], (d, h ^ i), MESH
         ).start()
     pltpu.make_async_copy(gain_ref, own_gains, recv_sem.at[2]).start()
+
+    pltpu.make_async_copy(win_hbm.at[0], win_buf, w_sem.at[1]).wait()
+    identity = (
+        lax.broadcasted_iota(I32, (256, 256), 0) == lax.broadcasted_iota(I32, (256, 256), 1)
+    ).astype(F32).astype(BF16)
+    for m in range(2):
+        for n in range(16):
+            part = win_buf[m, :, n * 256 : (n + 1) * 256]
+            turned[m, n * 256 : (n + 1) * 256, :] = lax.dot_general(
+                identity, part, nt, preferred_element_type=F32
+            ).astype(BF16)
 
     whole_wait(recv_m, recv_sem.at[1])
     messages = recv_m[...].astype(F32).reshape(64, 128).astype(BF16)
@@ -295,28 +294,17 @@
     select = select[:, :32].astype(BF16)
     pltpu.make_async_copy(wout_hbm, wout_buf, w_sem.at[0]).wait()
 
-    def project(half):
-        whole_wait(recv_a.at[half], half_sem.at[half])
-        rows_f[...] = recv_a[half].astype(F32).reshape(512, 128)
-        columns = jnp.zeros((64, 128), F32)
-        for n in range(4):
-            pair = [
-                jnp.concatenate(
-                    [rows_f[pl.ds(t * 8 + n * 2 + m, 32, stride=16), :] for t in range(2)], axis=0
-                )
-                for m in range(2)
-            ]
-            columns = columns + jnp.dot(
-                jnp.concatenate(pair, axis=1).astype(BF16),
-                wout_buf[n * 256 : (n + 1) * 256, :],
-                preferred_element_type=F32,
-            )
-        for t in range(2):
-            part_f[pl.ds(half * 2 + t, 32, stride=4), :] = columns[t * 32 : (t + 1) * 32]
-
-    project(0)
-    project(1)
-    part_buf[...] = part_f[...].astype(BF16).reshape(4, 32, 128)
+    whole_wait(recv_a, recv_sem.at[0])
+    rows_f[...] = recv_a[...].astype(F32).reshape(1024, 128)
+    columns = jnp.zeros((128, 128), F32)
+    for n in range(4):
+        pair = jnp.concatenate(
+            [rows_f[pl.ds(n * 2 + m, 128, stride=8), :] for m in range(2)], axis=1
+        ).astype(BF16)
+        columns = columns + jnp.dot(
+            pair, wout_buf[n * 256 : (n + 1) * 256, :], preferred_element_type=F32
+        )
+    part_buf[...] = columns.astype(BF16).reshape(4, 32, 128)
 
     for i in range(1, 4):
         to = h ^ i
@@ -377,7 +365,6 @@
                 MESH,
             ).start()
 
-    pltpu.make_async_copy(win_hbm.at[0], win_buf, w_sem.at[1]).wait()
     pltpu.make_async_copy(wdown_hbm.at[0], wdown_buf, w_sem.at[2]).wait()
     whole_wait(recv_g, recv_sem.at[2])
 
@@ -412,20 +399,20 @@
             x_buf[:, m * 128 : (m + 1) * 128] = (x * gains[m : m + 1]).astype(BF16)
         columns = pl.ds(pl.multiple_of(first * 1024, 1024), 1024)
         x = x_buf[...]
-        gate = gate + lax.dot_general(x, win_buf[0, :, columns], nt, preferred_element_type=F32)
-        up = up + lax.dot_general(x, win_buf[1, :, columns], nt, preferred_element_type=F32)
+        gate = gate + jnp.dot(x, turned[0, columns], preferred_element_type=F32)
+        up = up + jnp.dot(x, turned[1, columns], preferred_element_type=F32)
     inverse = lax.rsqrt(jnp.sum(squares, axis=1, keepdims=True) * (1.0 / 4096.0) + EPSILON)
     gate = gate * inverse
     hidden = (gate * jax.nn.sigmoid(gate) * (up * inverse)).astype(BF16)
 
-    def slab(side, core):
+    def slab(side, core, store):
         base = (side * 2 + core) * 1024
         for n in range(4):
             columns = pl.ds(pl.multiple_of(base + n * 256, 256), 256)
             part = jnp.dot(hidden, wdown_buf[:, columns], preferred_element_type=F32)
             for m in range(2):
-                slab_f[pl.ds(n * 2 + m, 64, stride=8), :] = part[:, m * 128 : (m + 1) * 128]
-        return slab_f[...]
+                store[pl.ds(n * 2 + m, 64, stride=8), :] = part[:, m * 128 : (m + 1) * 128]
+        return store[...]
 
     def to_sibling(side):
         return pltpu.make_async_remote_copy(
@@ -438,10 +425,10 @@
         )
 
     for side in range(2):
-        sib_buf[side] = slab(side, 1 - c).astype(BF16)
+        sib_buf[side] = slab(side, 1 - c, slab_f.at[side]).astype(BF16)
         to_sibling(side).start()
     for side in range(2):
-        own_f[side] = slab(side, c)
+        slab(side, c, own_f.at[side])
     for side in range(2):
         to_sibling(side).wait_recv()
         total = own_f[side] + recv_d[side].astype(F32)
@@ -495,8 +482,7 @@
 
     result = pltpu.make_async_copy(out_ref, out_hbm, w_sem.at[0])
     result.start()
-    for half in range(2):
-        whole_wait(recv_a.at[half, pl.ds(0, 31)], send_sem.at[0])
+    whole_wait(recv_a.at[pl.ds(0, 31)], send_sem.at[0])
 
     @pl.when(here)
     def _():
@@ -559,14 +545,14 @@
         + [
             pltpu.VMEM((1024, 128), BF16),
             pltpu.VMEM((2, 448, 4096), BF16),
+            pltpu.VMEM((2, 4096, 448), BF16),
             pltpu.VMEM((448, 4096), BF16),
-            pltpu.VMEM((2, 16, 128), BF16),
-            pltpu.VMEM((2, 32, 16, 128), BF16),
-            pltpu.VMEM((512, 128), F32),
+            pltpu.VMEM((32, 128), BF16),
+            pltpu.VMEM((32, 32, 128), BF16),
+            pltpu.VMEM((1024, 128), F32),
             pltpu.VMEM((8, 8, 128), BF16),
             pltpu.VMEM((8, 8, 128), BF16),
             pltpu.VMEM((32, 128), F32),
-            pltpu.VMEM((128, 128), F32),
             pltpu.VMEM((4, 32, 128), BF16),
             pltpu.VMEM((4, 32, 128), BF16),
             pltpu.VMEM((4, 8, 128), F32),
@@ -574,7 +560,7 @@
             pltpu.VMEM((2, 32, 2, 16, 128), BF16),
             pltpu.VMEM((8, 8, 128), F32),
             pltpu.VMEM((64, 1024), BF16),
-            pltpu.VMEM((512, 128), F32),
+            pltpu.VMEM((2, 512, 128), F32),
             pltpu.VMEM((2, 512, 128), F32),
             pltpu.VMEM((2, 512, 128), BF16),
             pltpu.VMEM((2, 512, 128), BF16),
@@ -586,7 +572,6 @@
             pltpu.SemaphoreType.DMA((3,)),
             pltpu.SemaphoreType.DMA((7,)),
             pltpu.SemaphoreType.DMA((7,)),
-            pltpu.SemaphoreType.DMA((2,)),
             pltpu.SemaphoreType.DMA((4,)),
             pltpu.SemaphoreType.DMA((4,)),
             pltpu.SemaphoreType.DMA((4,)),

time: 40.5 us -> 38.9 us (0.960)
  Pallas kernels: 39 us -> 37.3 us
    pallas_call x1, Pallas kernels: 39 us -> 37.3 us  [shards(): pl.pallas_call(layer, out_shape=jax.ShapeDtypeStruct((4, 1024), BF16), in...]
where the time goes in v5:
time: 38.9 us; the launch traced here: 38.6 us
  Pallas kernels  37.3 us (96%)
  local copies, waits for them, and re-layouts  1.3 us (3%)
    pallas_call x1, Pallas kernels, shards(): pl.pallas_call(layer, out_shape=jax.ShapeDtypeStruct((4, 1024), BF16), in...  37.3 us
    unnamed x1, local copies, waits for them, and re-layouts  1.3 us

profile of v5, /device:TPU:1, one launch (start us, length us, event | category | flops | bytes accessed | tf_op | source)
XLA Modules:
  0.0 38.6 jit_solution(519237754078265560)
XLA Ops:
  0.0 37.3 %layer.1 = bf16[4,1024]{1,0:T(4,128)(2,1)} custom-call(s32[2,4]{1,0:T(2,128)} %bitcast.10, f32[2,4]{1,0:T(2,128)} %bitcast.11, s32[4]{0:T(128)} %len_hbm.1, bf16[4,1024]{1,0:T(4,128)(2,1)} %residual_hbm.1, bf16[4,8,128]{2,1,0:T(8,128)(2,1)} %query_hbm.1, bf16[4,2,128]{2,1,0:T(2,128)(2,1)} %fresh_hbm.1, bf16[4,2,128]{2,1,0:T(2,128)(2,1)} %vnew_hbm.1, ...), custom_call_target="tpu_custom_call" | custom-call | tf_op jit(solution)/shard_map/layer/pallas_call | solution.py:526
  37.3 1.3 %copy.16 = bf16[4,1024]{1,0:T(4,128)(2,1)} copy(bf16[4,1024]{1,0:T(4,128)(2,1)} %layer.1) | data formatting | bytes 16384

commit v6 on v5

--- a/solution.py
+++ b/solution.py
@@ -16,6 +16,7 @@
 MESH = pl.DeviceIdType.MESH
 FAR = sorted(range(1, 32), key=lambda i: -(2 * (i >> 4) + (0, 1, 2, 1)[i >> 2 & 3] + (0, 1, 2, 1)[i & 3]))
 ORDER = (0, 1, 2, 3)
+SEND_B = sorted(FAR + [0], key=lambda i: i >> 3)
 OUT_SPACE = pl.ANY
 
 
@@ -306,7 +307,7 @@
         )
     part_buf[...] = columns.astype(BF16).reshape(4, 32, 128)
 
-    for i in range(1, 4):
+    for i in (3, 2, 1):
         to = h ^ i
         pltpu.make_async_remote_copy(
             part_buf.at[to], recv_r.at[h], send_sem.at[3], recv_sem.at[3], (d, to), MESH
@@ -324,7 +325,7 @@
     )
 
     slot = block
-    for i in range(32):
+    for i in SEND_B:
         to = d ^ i
         for side in range(2):
             place = recv_b.at[c, (i & 24) + slot, y]

time: 38.9 us -> 38.7 us (level)
  no operation moved by 1% of the time
where the time goes in v6:
time: 38.7 us; the launch traced here: 38.5 us
  Pallas kernels  37.1 us (96%)
  local copies, waits for them, and re-layouts  1.3 us (3%)
    pallas_call x1, Pallas kernels, shards(): pl.pallas_call(layer, out_shape=jax.ShapeDtypeStruct((4, 1024), BF16), in...  37.1 us
    unnamed x1, local copies, waits for them, and re-layouts  1.3 us

profile of v6, /device:TPU:1, one launch (start us, length us, event | category | flops | bytes accessed | tf_op | source)
XLA Modules:
  0.0 38.5 jit_solution(7111470132476237398)
XLA Ops:
  0.0 37.1 %layer.1 = bf16[4,1024]{1,0:T(4,128)(2,1)} custom-call(s32[2,4]{1,0:T(2,128)} %bitcast.10, f32[2,4]{1,0:T(2,128)} %bitcast.11, s32[4]{0:T(128)} %len_hbm.1, bf16[4,1024]{1,0:T(4,128)(2,1)} %residual_hbm.1, bf16[4,8,128]{2,1,0:T(8,128)(2,1)} %query_hbm.1, bf16[4,2,128]{2,1,0:T(2,128)(2,1)} %fresh_hbm.1, bf16[4,2,128]{2,1,0:T(2,128)(2,1)} %vnew_hbm.1, ...), custom_call_target="tpu_custom_call" | custom-call | tf_op jit(solution)/shard_map/layer/pallas_call | solution.py:527
  37.2 1.3 %copy.16 = bf16[4,1024]{1,0:T(4,128)(2,1)} copy(bf16[4,1024]{1,0:T(4,128)(2,1)} %layer.1) | data formatting | bytes 16384

commit v7 on v6

--- a/solution.py
+++ b/solution.py
@@ -272,12 +272,15 @@
     identity = (
         lax.broadcasted_iota(I32, (256, 256), 0) == lax.broadcasted_iota(I32, (256, 256), 1)
     ).astype(F32).astype(BF16)
-    for m in range(2):
+
+    def turn(m):
         for n in range(16):
             part = win_buf[m, :, n * 256 : (n + 1) * 256]
             turned[m, n * 256 : (n + 1) * 256, :] = lax.dot_general(
                 identity, part, nt, preferred_element_type=F32
             ).astype(BF16)
+
+    turn(0)
 
     whole_wait(recv_m, recv_sem.at[1])
     messages = recv_m[...].astype(F32).reshape(64, 128).astype(BF16)
@@ -313,6 +316,7 @@
             part_buf.at[to], recv_r.at[h], send_sem.at[3], recv_sem.at[3], (d, to), MESH
         ).start()
     pltpu.make_async_copy(part_buf.at[h], recv_r.at[h], recv_sem.at[3]).start()
+    turn(1)
     whole_wait(recv_r, recv_sem.at[3])
     stream = residual
     for i in range(4):

time: 38.7 us -> 38.7 us (level)
  no operation moved by 1% of the time
where the time goes in v7:
time: 38.7 us; the launch traced here: 38.5 us
  Pallas kernels  37.2 us (96%)
  local copies, waits for them, and re-layouts  1.3 us (3%)
    pallas_call x1, Pallas kernels, shards(): pl.pallas_call(layer, out_shape=jax.ShapeDtypeStruct((4, 1024), BF16), in...  37.2 us
    unnamed x1, local copies, waits for them, and re-layouts  1.3 us

profile of v7, /device:TPU:1, one launch (start us, length us, event | category | flops | bytes accessed | tf_op | source)
XLA Modules:
  0.0 38.5 jit_solution(10496410929688822687)
XLA Ops:
  0.0 37.2 %layer.1 = bf16[4,1024]{1,0:T(4,128)(2,1)} custom-call(s32[2,4]{1,0:T(2,128)} %bitcast.10, f32[2,4]{1,0:T(2,128)} %bitcast.11, s32[4]{0:T(128)} %len_hbm.1, bf16[4,1024]{1,0:T(4,128)(2,1)} %residual_hbm.1, bf16[4,8,128]{2,1,0:T(8,128)(2,1)} %query_hbm.1, bf16[4,2,128]{2,1,0:T(2,128)(2,1)} %fresh_hbm.1, bf16[4,2,128]{2,1,0:T(2,128)(2,1)} %vnew_hbm.1, ...), custom_call_target="tpu_custom_call" | custom-call | tf_op jit(solution)/shard_map/layer/pallas_call | solution.py:531
  37.2 1.3 %copy.16 = bf16[4,1024]{1,0:T(4,128)(2,1)} copy(bf16[4,1024]{1,0:T(4,128)(2,1)} %layer.1) | data formatting | bytes 16384
